TPU v7x, 256 devices: a whole 4x4x8 slice. The times are simulated.
256 devices in a mesh: seq: 64 (over z, y, core), tp: 4 (over x).
Axes of the slice: x: 4, y: 4, z: 8, core: 2. Of those that a mesh axis runs over, the one named last changes fastest.
Arguments:
- q_new: bfloat16 [32768, 8192], P('seq', 'tp'), may hold values from -16 to 16
- k_new: bfloat16 [32768, 1024], P('seq', 'tp'), may hold values from -6 to 6
- v_new: bfloat16 [32768, 1024], P('seq', 'tp'), may hold values from -6 to 6
- q_bias: bfloat16 [8192], P('tp'), may hold values from -3 to 3
- k_bias: bfloat16 [1024], P('tp'), may hold values from -3 to 3
- v_bias: bfloat16 [1024], P('tp'), may hold values from -3 to 3
- cache_k: bfloat16 [131072, 1024], P('seq', 'tp'), may hold values from -16 to 16
- cache_v: bfloat16 [131072, 1024], P('seq', 'tp'), may hold values from -6 to 6
- deal: int32 [64], replicated, may hold values from 0 to 63, each once
- cache_len: int32 [64], replicated, may hold values from 1 to 2048, 65536 in all
Outputs:
- attn_out: bfloat16 [32768, 8192], P('seq', 'tp')
- new_keys: bfloat16 [32768, 1024], P('seq', 'tp')
- new_values: bfloat16 [32768, 1024], P('seq', 'tp')
- last_norm: float32 [64], P('seq')
- top_logit: float32 [64], P('seq')
Inputs may be any that keep to these rules, and one draw needn't show every extreme that they name: `deal`: each request fills exactly one slot. `cache_len`: the lengths sum to 65536 and the largest is exactly 2048.
All inputs are finite; a program needn't handle non-finite values.
Results may differ from a plain program's by a relative error of at most 0.012.
Values may be sent and summed in bfloat16 or wider, within the bound.
A program may use at most 192 MiB of HBM per device.

v0:
```python
import math

import jax
import jax.numpy as jnp
from jax import lax
from jax.sharding import PartitionSpec as P

HEAD = 128


theta_base = 1000000.0
masked_score = -1e30
norm_epsilon = 1e-06


def rotate(vectors, positions):
    half_dim = vectors.shape[-1] // 2
    frequency = theta_base ** (-2.0 * jnp.arange(half_dim, dtype=jnp.float32) / vectors.shape[-1])
    angles = positions.astype(jnp.float32)[:, None] * frequency[None, :]
    cosine = jnp.cos(angles)[:, None, :]
    sine_part = jnp.sin(angles)[:, None, :]
    lower_part = vectors[..., :half_dim]
    upper_part = vectors[..., half_dim:]
    return jnp.concatenate(
        [
            lower_part * cosine - upper_part * sine_part,
            upper_part * cosine + lower_part * sine_part,
        ],
        axis=-1,
    )


def prepare(q_raw, k_raw, v_raw, q_bias, k_bias, v_bias, length):
    row_count = q_raw.shape[0]
    head_count = q_raw.shape[1] // HEAD
    kv_count = k_raw.shape[1] // HEAD
    positions = length + jnp.arange(row_count, dtype=jnp.int32)
    queries = rotate(
        (q_raw.astype(jnp.float32) + q_bias.astype(jnp.float32)).reshape(
            row_count, head_count, HEAD
        ),
        positions,
    ).astype(jnp.bfloat16)
    fresh_keys = rotate(
        (k_raw.astype(jnp.float32) + k_bias.astype(jnp.float32)).reshape(row_count, kv_count, HEAD),
        positions,
    ).astype(jnp.bfloat16)
    fresh_values = (
        (v_raw.astype(jnp.float32) + v_bias.astype(jnp.float32))
        .astype(jnp.bfloat16)
        .reshape(row_count, kv_count, HEAD)
    )
    return (
        queries.reshape(row_count, kv_count, head_count // kv_count, HEAD),
        fresh_keys,
        fresh_values,
    )


def fresh_state(queries):
    row_count, kv_count, group, head_dim = queries.shape
    return (
        jnp.full((kv_count, group, row_count), masked_score, jnp.float32),
        jnp.zeros((kv_count, group, row_count), jnp.float32),
        jnp.zeros((kv_count, group, row_count, head_dim), jnp.float32),
    )


def attend_block(carry_state, queries, key_rows, value_rows, valid):
    running_max, running_sum, weighted = carry_state
    scores = jnp.einsum(
        "qkgd,tkd->kgqt", queries, key_rows, preferred_element_type=jnp.float32
    ) * HEAD ** (-0.5)
    scores = jnp.where(valid, scores, masked_score)
    new_max = jnp.maximum(running_max, jnp.max(scores, axis=-1))
    weight = jnp.where(valid, jnp.exp(scores - new_max[..., None]), 0.0)
    factor = jnp.exp(running_max - new_max)
    new_sum = running_sum * factor + jnp.sum(weight, axis=-1)
    new_weighted = weighted * factor[..., None] + jnp.einsum(
        "kgqt,tkd->kgqd",
        weight.astype(jnp.bfloat16),
        value_rows,
        preferred_element_type=jnp.float32,
    )
    return (new_max, new_sum, new_weighted)


def attend_cache(carry_state, queries, stored_k, stored_v, valid_rows):
    buffer_rows = stored_k.shape[0]
    kv_count = queries.shape[1]
    block_rows = math.gcd(512, buffer_rows)

    def advance(index, inner_state):
        first_row = index * block_rows
        key_rows = lax.dynamic_slice_in_dim(stored_k, first_row, block_rows, 0).reshape(
            block_rows, kv_count, HEAD
        )
        value_rows = lax.dynamic_slice_in_dim(stored_v, first_row, block_rows, 0).reshape(
            block_rows, kv_count, HEAD
        )
        valid = first_row + jnp.arange(block_rows, dtype=jnp.int32) < valid_rows
        return attend_block(inner_state, queries, key_rows, value_rows, valid[None, None, None, :])

    block_total = (valid_rows + block_rows - 1) // block_rows
    return lax.fori_loop(0, block_total, advance, carry_state)


def split_rows(matrix, slot_count):
    return matrix.reshape(slot_count, matrix.shape[0] // slot_count, matrix.shape[1])


def body(q_new, k_new, v_new, q_bias, k_bias, v_bias, cache_k, cache_v, deal, cache_len):
    slot_count = lax.axis_size("seq")
    own_slot = lax.axis_index("seq")
    slot_ids = jnp.arange(slot_count, dtype=jnp.int32)
    inverse = jnp.sum(jnp.where(deal[None, :] == slot_ids[:, None], slot_ids[None, :], 0), axis=1)
    spread = (
        lax.all_to_all(
            split_rows(q_new, slot_count), "seq", split_axis=0, concat_axis=0, tiled=True
        ),
        lax.all_to_all(
            split_rows(k_new, slot_count), "seq", split_axis=0, concat_axis=0, tiled=True
        ),
        lax.all_to_all(
            split_rows(v_new, slot_count), "seq", split_axis=0, concat_axis=0, tiled=True
        ),
    )
    picked = (
        jnp.take(spread[0], inverse, axis=0),
        jnp.take(spread[1], inverse, axis=0),
        jnp.take(spread[2], inverse, axis=0),
    )
    settled = (
        lax.all_to_all(picked[0], "seq", split_axis=0, concat_axis=0, tiled=True),
        lax.all_to_all(picked[1], "seq", split_axis=0, concat_axis=0, tiled=True),
        lax.all_to_all(picked[2], "seq", split_axis=0, concat_axis=0, tiled=True),
    )
    tok_q = settled[0].reshape(q_new.shape)
    tok_k = settled[1].reshape(k_new.shape)
    tok_v = settled[2].reshape(v_new.shape)
    local_k, local_v = (cache_k, cache_v)
    request = slot_ids[own_slot]
    length = cache_len[request]
    queries, fresh_keys, fresh_values = prepare(tok_q, tok_k, tok_v, q_bias, k_bias, v_bias, length)
    row_count = queries.shape[0]
    carry_state = attend_cache(fresh_state(queries), queries, local_k, local_v, length)
    causal = (
        jnp.arange(row_count, dtype=jnp.int32)[None, :]
        <= jnp.arange(row_count, dtype=jnp.int32)[:, None]
    )
    carry_state = attend_block(
        carry_state, queries, fresh_keys, fresh_values, causal[None, None, :, :]
    )
    mixture = (
        (carry_state[2] / carry_state[1][..., None]).transpose(2, 0, 1, 3).reshape(row_count, -1)
    )
    last_row = mixture[row_count - 1]
    squares = lax.psum(jnp.sum(last_row * last_row), "tp")
    feature_count = mixture.shape[1] * lax.axis_size("tp")
    norm_value = jnp.sqrt(squares / feature_count + norm_epsilon)
    top_value = lax.pmax(jnp.max(carry_state[0][:, :, row_count - 1]), "tp")
    attn_local = mixture.astype(jnp.bfloat16)
    keys_local = fresh_keys.reshape(row_count, -1)
    values_local = fresh_values.reshape(row_count, -1)
    attn_out, new_keys, new_values = (attn_local, keys_local, values_local)
    last_norm = norm_value.reshape(1)
    top_logit = top_value.reshape(1)
    return (attn_out, new_keys, new_values, last_norm, top_logit)


def solution(mesh):
    return jax.shard_map(
        body,
        mesh=mesh,
        in_specs=(
            P("seq", "tp"),
            P("seq", "tp"),
            P("seq", "tp"),
            P("tp"),
            P("tp"),
            P("tp"),
            P("seq", "tp"),
            P("seq", "tp"),
            P(),
            P(),
        ),
        out_specs=(P("seq", "tp"), P("seq", "tp"), P("seq", "tp"), P("seq"), P("seq")),
        check_vma=False,
    )
```

profile of v0, /device:TPU:18, one launch (start us, length us, event | category | flops | bytes accessed | tf_op | source)
XLA Modules:
  0.0 337.7 jit_solution(14504451122693815724)
XLA Ops:
  0.6 23.9 %all_to_all.30 = bf16[64,8,256]{2,1,0:T(8,128)(2,1)S(1)} all-to-all(bf16[64,8,256]{2,1,0:T(8,128)(2,1)} %bitcast.108), channel_id=1, replica_groups=mesh['seq'=64,'tp'=4] {'seq'}, dimensions={0} | all-to-all | bytes 524288 | tf_op jit(solution)/shard_map/all_to_all | solution.py:121
  24.6 17.9 %all_to_all.31 = bf16[64,8,256]{2,1,0:T(8,128)(2,1)S(1)} all-to-all(bf16[64,8,256]{2,1,0:T(8,128)(2,1)} %bitcast.109), channel_id=1, replica_groups=mesh['seq'=64,'tp'=4] {'seq'}, dimensions={0} | all-to-all | bytes 524288 | tf_op jit(solution)/shard_map/all_to_all | solution.py:124
  42.5 5.9 %all-to-all-start = ((bf16[64,8,2048]{2,1,0:T(8,128)(2,1)}), bf16[64,8,2048]{2,1,0:T(8,128)(2,1)S(1)}, u32[]{:S(2)}, u32[]{:S(2)}) async-start(bf16[64,8,2048]{2,1,0:T(8,128)(2,1)} %bitcast.106), calls=%async_computation | async-start | bytes 4194304 | tf_op jit(solution)/shard_map/all_to_all | solution.py:118
  50.7 49.0 %all-to-all-done = bf16[64,8,2048]{2,1,0:T(8,128)(2,1)S(1)} async-done(((bf16[64,8,2048]{2,1,0:T(8,128)(2,1)}), bf16[64,8,2048]{2,1,0:T(8,128)(2,1)S(1)}, u32[]{:S(2)}, u32[]{:S(2)}) %all-to-all-start) | async-done | bytes 2097184 | tf_op jit(solution)/shard_map/all_to_all | solution.py:118
  99.7 5.4 %all-to-all-start.5 = ((bf16[64,8,256]{2,1,0:T(8,128)(2,1)}), bf16[64,8,256]{2,1,0:T(8,128)(2,1)S(1)}, u32[]{:S(2)}, u32[]{:S(2)}) async-start(bf16[64,8,256]{2,1,0:T(8,128)(2,1)} %get-tuple-element.121), calls=%async_computation.5 | async-start | bytes 524288 | tf_op jit(solution)/shard_map/all_to_all | solution.py:136
  107.1 9.9 %all-to-all-done.5 = bf16[64,8,256]{2,1,0:T(8,128)(2,1)S(1)} async-done(((bf16[64,8,256]{2,1,0:T(8,128)(2,1)}), bf16[64,8,256]{2,1,0:T(8,128)(2,1)S(1)}, u32[]{:S(2)}, u32[]{:S(2)}) %all-to-all-start.5) | async-done | bytes 262176 | tf_op jit(solution)/shard_map/all_to_all | solution.py:136
  117.0 5.9 %all-to-all-start.3 = ((bf16[64,8,256]{2,1,0:T(8,128)(2,1)}), bf16[64,8,256]{2,1,0:T(8,128)(2,1)S(1)}, u32[]{:S(2)}, u32[]{:S(2)}) async-start(bf16[64,8,256]{2,1,0:T(8,128)(2,1)} %get-tuple-element.122), calls=%async_computation.3 | async-start | bytes 524288 | tf_op jit(solution)/shard_map/all_to_all | solution.py:135
  123.0 3.2 broadcast_select_fusion
  126.2 8.7 %all-to-all-done.3 = bf16[64,8,256]{2,1,0:T(8,128)(2,1)S(1)} async-done(((bf16[64,8,256]{2,1,0:T(8,128)(2,1)}), bf16[64,8,256]{2,1,0:T(8,128)(2,1)S(1)}, u32[]{:S(2)}, u32[]{:S(2)}) %all-to-all-start.3) | async-done | bytes 262176 | tf_op jit(solution)/shard_map/all_to_all | solution.py:135
  134.9 5.9 %all-to-all-start.1 = ((bf16[64,8,2048]{2,1,0:T(8,128)(2,1)}), bf16[64,8,2048]{2,1,0:T(8,128)(2,1)S(1)}, u32[]{:S(2)}, u32[]{:S(2)}) async-start(bf16[64,8,2048]{2,1,0:T(8,128)(2,1)} %broadcast_select_fusion), calls=%async_computation.1 | async-start | bytes 4194304 | tf_op jit(solution)/shard_map/all_to_all | solution.py:134
  151.9 40.2 %all-to-all-done.1 = bf16[64,8,2048]{2,1,0:T(8,128)(2,1)S(1)} async-done(((bf16[64,8,2048]{2,1,0:T(8,128)(2,1)}), bf16[64,8,2048]{2,1,0:T(8,128)(2,1)S(1)}, u32[]{:S(2)}, u32[]{:S(2)}) %all-to-all-start.1) | async-done | bytes 2097184 | tf_op jit(solution)/shard_map/all_to_all | solution.py:134
  201.3 84.2 %while.14 = (s32[]{:T(128)}, f32[2,8,512]{2,1,0:T(8,128)}, f32[2,8,512]{2,1,0:T(8,128)}, f32[2,8,512,128]{3,2,1,0:T(8,128)}, s32[]{:T(128)}, /*index=5*/s32[]{:T...) while((s32[]{:T(128)}, f32[2,8,512]{2,1,0:T(8,128)}, ...), condition=%wide.region_4.5_spmd, body=%wide.region_1.0_spmd.sunk | while | flops 2204124160 | bytes 64358664 | solution.py:105
  203.4 4.2 %bitcast_reduce_fusion.2 = (f32[2,8,512]{2,1,0:T(8,128)S(1)}, f32[2,512,512,8]{2,1,3,0:T(8,128)S(1)}) fusion(pred[512]{0:T(512)(128)(4,1)S(1)} %add_compare_fusion.2, bf16[512,2,128,1]{0,2,3,1:T(8,128)(2,1)S(1)} %bitcast.101, bf16[512,2,8,128]{3,0,2,1:T(8,128)(2,1)S(1)} %get-tuple-element.228), kind=kOutput, calls=%fused_computation.4.clone.1 | convolution fusion | flops 1086316544 | bytes 19169792 | tf_op jit(solution)/shard_map/while/body/qkgd,tkd->kgqt/dot_general | solution.py:71
  207.6 4.6 %fusion.46 = f32[2,8,512]{2,1,0:T(8,128)S(1)} fusion(f32[2,512,512,8]{2,1,3,0:T(8,128)S(1)} %get-tuple-element.191, f32[2,8,512]{2,1,0:T(8,128)S(1)} %max.10, pred[512]{0:T(512)(128)(4,1)S(1)} %add_compare_fusion.2), kind=kLoop, calls=%fused_computation.9.clone.1 | loop fusion | flops 20963328 | bytes 16843264 | tf_op jit(solution)/shard_map/while/body/reduce_sum | solution.py:78
  212.3 9.5 %multiply_add_fusion.7 = f32[2,8,512,128]{3,2,1,0:T(8,128)} fusion(f32[2,8,512,128]{3,2,1,0:T(8,128)} %get-tuple-element.211, f32[2,8,512]{2,1,0:T(8,128)S(1)} %get-tuple-element.193, bf16[512,2,128,1]{0,2,3,1:T(8,128)(2,1)S(1)} %bitcast.105, f32[2,512,512,8]{2,1,3,0:T(8,128)S(1)} %get-tuple-element.191, f32[2,8,512]{2,1,0:T(8,128)S(1)} %max.10, ...), kind=kOutput, calls=%fused_computation.13.clone.1 | convolution fusion | flops 1096810496 | bytes 25494016 | tf_op jit(solution)/shard_map/while/body/kgqt,tkd->kgqd/dot_general | solution.py:79
  224.4 4.2 %bitcast_reduce_fusion.2 = (f32[2,8,512]{2,1,0:T(8,128)S(1)}, f32[2,512,512,8]{2,1,3,0:T(8,128)S(1)}) fusion(pred[512]{0:T(512)(128)(4,1)S(1)} %add_compare_fusion.2, bf16[512,2,128,1]{0,2,3,1:T(8,128)(2,1)S(1)} %bitcast.101, bf16[512,2,8,128]{3,0,2,1:T(8,128)(2,1)S(1)} %get-tuple-element.228), kind=kOutput, calls=%fused_computation.4.clone.1 | convolution fusion | flops 1086316544 | bytes 19169792 | tf_op jit(solution)/shard_map/while/body/qkgd,tkd->kgqt/dot_general | solution.py:71
  228.7 4.6 %fusion.46 = f32[2,8,512]{2,1,0:T(8,128)S(1)} fusion(f32[2,512,512,8]{2,1,3,0:T(8,128)S(1)} %get-tuple-element.191, f32[2,8,512]{2,1,0:T(8,128)S(1)} %max.10, pred[512]{0:T(512)(128)(4,1)S(1)} %add_compare_fusion.2), kind=kLoop, calls=%fused_computation.9.clone.1 | loop fusion | flops 20963328 | bytes 16843264 | tf_op jit(solution)/shard_map/while/body/reduce_sum | solution.py:78
  233.4 9.5 %multiply_add_fusion.7 = f32[2,8,512,128]{3,2,1,0:T(8,128)} fusion(f32[2,8,512,128]{3,2,1,0:T(8,128)} %get-tuple-element.211, f32[2,8,512]{2,1,0:T(8,128)S(1)} %get-tuple-element.193, bf16[512,2,128,1]{0,2,3,1:T(8,128)(2,1)S(1)} %bitcast.105, f32[2,512,512,8]{2,1,3,0:T(8,128)S(1)} %get-tuple-element.191, f32[2,8,512]{2,1,0:T(8,128)S(1)} %max.10, ...), kind=kOutput, calls=%fused_computation.13.clone.1 | convolution fusion | flops 1096810496 | bytes 25494016 | tf_op jit(solution)/shard_map/while/body/kgqt,tkd->kgqd/dot_general | solution.py:79
  245.5 4.2 %bitcast_reduce_fusion.2 = (f32[2,8,512]{2,1,0:T(8,128)S(1)}, f32[2,512,512,8]{2,1,3,0:T(8,128)S(1)}) fusion(pred[512]{0:T(512)(128)(4,1)S(1)} %add_compare_fusion.2, bf16[512,2,128,1]{0,2,3,1:T(8,128)(2,1)S(1)} %bitcast.101, bf16[512,2,8,128]{3,0,2,1:T(8,128)(2,1)S(1)} %get-tuple-element.228), kind=kOutput, calls=%fused_computation.4.clone.1 | convolution fusion | flops 1086316544 | bytes 19169792 | tf_op jit(solution)/shard_map/while/body/qkgd,tkd->kgqt/dot_general | solution.py:71
  249.7 4.6 %fusion.46 = f32[2,8,512]{2,1,0:T(8,128)S(1)} fusion(f32[2,512,512,8]{2,1,3,0:T(8,128)S(1)} %get-tuple-element.191, f32[2,8,512]{2,1,0:T(8,128)S(1)} %max.10, pred[512]{0:T(512)(128)(4,1)S(1)} %add_compare_fusion.2), kind=kLoop, calls=%fused_computation.9.clone.1 | loop fusion | flops 20963328 | bytes 16843264 | tf_op jit(solution)/shard_map/while/body/reduce_sum | solution.py:78
  254.4 9.5 %multiply_add_fusion.7 = f32[2,8,512,128]{3,2,1,0:T(8,128)} fusion(f32[2,8,512,128]{3,2,1,0:T(8,128)} %get-tuple-element.211, f32[2,8,512]{2,1,0:T(8,128)S(1)} %get-tuple-element.193, bf16[512,2,128,1]{0,2,3,1:T(8,128)(2,1)S(1)} %bitcast.105, f32[2,512,512,8]{2,1,3,0:T(8,128)S(1)} %get-tuple-element.191, f32[2,8,512]{2,1,0:T(8,128)S(1)} %max.10, ...), kind=kOutput, calls=%fused_computation.13.clone.1 | convolution fusion | flops 1096810496 | bytes 25494016 | tf_op jit(solution)/shard_map/while/body/kgqt,tkd->kgqd/dot_general | solution.py:79
  266.5 4.2 %bitcast_reduce_fusion.2 = (f32[2,8,512]{2,1,0:T(8,128)S(1)}, f32[2,512,512,8]{2,1,3,0:T(8,128)S(1)}) fusion(pred[512]{0:T(512)(128)(4,1)S(1)} %add_compare_fusion.2, bf16[512,2,128,1]{0,2,3,1:T(8,128)(2,1)S(1)} %bitcast.101, bf16[512,2,8,128]{3,0,2,1:T(8,128)(2,1)S(1)} %get-tuple-element.228), kind=kOutput, calls=%fused_computation.4.clone.1 | convolution fusion | flops 1086316544 | bytes 19169792 | tf_op jit(solution)/shard_map/while/body/qkgd,tkd->kgqt/dot_general | solution.py:71
  270.8 4.6 %fusion.46 = f32[2,8,512]{2,1,0:T(8,128)S(1)} fusion(f32[2,512,512,8]{2,1,3,0:T(8,128)S(1)} %get-tuple-element.191, f32[2,8,512]{2,1,0:T(8,128)S(1)} %max.10, pred[512]{0:T(512)(128)(4,1)S(1)} %add_compare_fusion.2), kind=kLoop, calls=%fused_computation.9.clone.1 | loop fusion | flops 20963328 | bytes 16843264 | tf_op jit(solution)/shard_map/while/body/reduce_sum | solution.py:78
  275.5 9.5 %multiply_add_fusion.7 = f32[2,8,512,128]{3,2,1,0:T(8,128)} fusion(f32[2,8,512,128]{3,2,1,0:T(8,128)} %get-tuple-element.211, f32[2,8,512]{2,1,0:T(8,128)S(1)} %get-tuple-element.193, bf16[512,2,128,1]{0,2,3,1:T(8,128)(2,1)S(1)} %bitcast.105, f32[2,512,512,8]{2,1,3,0:T(8,128)S(1)} %get-tuple-element.191, f32[2,8,512]{2,1,0:T(8,128)S(1)} %max.10, ...), kind=kOutput, calls=%fused_computation.13.clone.1 | convolution fusion | flops 1096810496 | bytes 25494016 | tf_op jit(solution)/shard_map/while/body/kgqt,tkd->kgqd/dot_general | solution.py:79
  285.6 3.9 %fusion.13 = (f32[2,8,512]{2,1,0:T(8,128)S(1)}, f32[2,512,512,8]{2,1,3,0:T(8,128)S(1)}) fusion(pred[512,512]{0,1:T(8,128)(4,1)} %iota_compare_fusion, bf16[512,2,8,128]{3,0,2,1:T(8,128)(2,1)S(1)} %get-tuple-element.234, bf16[512,2,128]{2,0,1:T(8,128)(2,1)} %copy-done.5), kind=kOutput, calls=%fused_computation.24 | convolution fusion | flops 1086316544 | bytes 19431424 | tf_op jit(solution)/shard_map/qkgd,tkd->kgqt/dot_general | solution.py:71
  290.3 4.9 %copy-done = f32[2,512,512,8]{2,1,3,0:T(8,128)} copy-done((f32[2,512,512,8]{2,1,3,0:T(8,128)}, f32[2,512,512,8]{2,1,3,0:T(8,128)S(1)}, u32[]{:S(2)}) %copy-start) | copy-done | bytes 16777240
  295.2 4.0 %fusion.14 = f32[2,8,512]{2,1,0:T(8,128)S(1)} fusion(f32[2,512,512,8]{2,1,3,0:T(8,128)S(1)} %get-tuple-element.124, f32[2,8,512]{2,1,0:T(8,128)S(1)} %max.8, pred[512,512]{0,1:T(8,128)(4,1)S(1)} %copy-done.3), kind=kLoop, calls=%fused_computation.25 | loop fusion | flops 20963328 | bytes 17104896 | tf_op jit(solution)/shard_map/reduce_sum | solution.py:78
  299.3 10.8 %fusion.32 = (bf16[512,2,8,128]{3,0,2,1:T(8,128)(2,1)}, f32[512,2,8,128]{3,0,2,1:T(8,128)S(1)}) fusion(f32[2,8,512]{2,1,0:T(8,128)S(1)} %get-tuple-element.107, bf16[512,2,128,1]{2,1,0,3:T(2,128)(2,1)S(1)} %copy-done.9, f32[2,512,512,8]{2,1,3,0:T(8,128)} %copy-done, f32[2,8,512]{2,1,0:T(8,128)S(1)} %max.8, pred[512,512]{0,1:T(8,128)(4,1)S(1)} %copy-done.3, ...), kind=kOutput, calls=%fused_computation.74 | convolution fusion | flops 1098907648 | bytes 27885568 | tf_op jit(solution)/shard_map/kgqt,tkd->kgqd/dot_general | solution.py:79
  310.7 9.2 %pmax.7 = f32[1]{0:T(128)} all-reduce(f32[1]{0:T(128)} %bitcast.25), channel_id=1, replica_groups=mesh['seq'=64,'tp'=4] {'tp'}, use_global_device_ids=true, to_apply=%region_10.12 | all-reduce | flops 1 | bytes 8 | tf_op jit(solution)/shard_map/pmax | solution.py:161
  319.9 10.7 %psum.7 = f32[]{:T(128)} all-reduce(f32[]{:T(128)} %fusion.26), channel_id=1, replica_groups=mesh['seq'=64,'tp'=4] {'tp'}, use_global_device_ids=true, to_apply=%region_8.10 | all-reduce | flops 1 | bytes 8 | tf_op jit(solution)/shard_map/psum | solution.py:158
  331.3 2.9 copy.41
  334.2 2.4 copy.43
  (116 shorter events, 35.9 us)
Async XLA Ops:
  0.6 47.8 %copy-start.12 = (s32[64]{0:T(128)S(1)}, s32[64]{0:T(128)}, u32[]{:S(2)}) copy-start(s32[64]{0:T(128)} %param.22) | copy-start | bytes 772
  42.5 57.2 %all-to-all-start = ((bf16[64,8,2048]{2,1,0:T(8,128)(2,1)}), bf16[64,8,2048]{2,1,0:T(8,128)(2,1)S(1)}, u32[]{:S(2)}, u32[]{:S(2)}) async-start(bf16[64,8,2048]{2,1,0:T(8,128)(2,1)} %bitcast.106), calls=%async_computation | async-start | bytes 4194304 | tf_op jit(solution)/shard_map/all_to_all | solution.py:118
  99.7 17.4 %all-to-all-start.5 = ((bf16[64,8,256]{2,1,0:T(8,128)(2,1)}), bf16[64,8,256]{2,1,0:T(8,128)(2,1)S(1)}, u32[]{:S(2)}, u32[]{:S(2)}) async-start(bf16[64,8,256]{2,1,0:T(8,128)(2,1)} %get-tuple-element.121), calls=%async_computation.5 | async-start | bytes 524288 | tf_op jit(solution)/shard_map/all_to_all | solution.py:136
  117.0 17.9 %all-to-all-start.3 = ((bf16[64,8,256]{2,1,0:T(8,128)(2,1)}), bf16[64,8,256]{2,1,0:T(8,128)(2,1)S(1)}, u32[]{:S(2)}, u32[]{:S(2)}) async-start(bf16[64,8,256]{2,1,0:T(8,128)(2,1)} %get-tuple-element.122), calls=%async_computation.3 | async-start | bytes 524288 | tf_op jit(solution)/shard_map/all_to_all | solution.py:135
  123.0 17.9 %copy-start.13 = (s32[64]{0:T(128)S(1)}, s32[64]{0:T(128)}, u32[]{:S(2)}) copy-start(s32[64]{0:T(128)} %param.23) | copy-start | bytes 772
  123.0 20.6 %copy-start.14 = (bf16[256]{0:T(256)(128)(2,1)S(1)}, bf16[256]{0:T(256)(128)(2,1)}, u32[]{:S(2)}) copy-start(bf16[256]{0:T(256)(128)(2,1)} %param.18) | copy-start | bytes 1540
  123.0 20.6 %copy-start.11 = (bf16[256]{0:T(256)(128)(2,1)S(1)}, bf16[256]{0:T(256)(128)(2,1)}, u32[]{:S(2)}) copy-start(bf16[256]{0:T(256)(128)(2,1)} %param.19) | copy-start | bytes 1540
  123.0 20.6 %copy-start.10 = (bf16[2048]{0:T(1024)(128)(2,1)S(1)}, bf16[2048]{0:T(1024)(128)(2,1)}, u32[]{:S(2)}) copy-start(bf16[2048]{0:T(1024)(128)(2,1)} %param.17) | copy-start | bytes 12292
  134.9 57.2 %all-to-all-start.1 = ((bf16[64,8,2048]{2,1,0:T(8,128)(2,1)}), bf16[64,8,2048]{2,1,0:T(8,128)(2,1)S(1)}, u32[]{:S(2)}, u32[]{:S(2)}) async-start(bf16[64,8,2048]{2,1,0:T(8,128)(2,1)} %broadcast_select_fusion), calls=%async_computation.1 | async-start | bytes 4194304 | tf_op jit(solution)/shard_map/all_to_all | solution.py:134
  147.2 45.5 %copy-start.5 = (bf16[512,2,128]{2,0,1:T(8,128)(2,1)}, bf16[512,2,128]{2,0,1:T(8,128)(2,1)S(1)}, u32[]{:S(2)}) copy-start(bf16[512,2,128]{2,0,1:T(8,128)(2,1)S(1)} %maximum_convert_fusion) | copy-start | bytes 786436
  203.4 4.2 %copy-start.1 = (f32[2,8,512]{2,1,0:T(8,128)S(1)}, f32[2,8,512]{2,1,0:T(8,128)}, u32[]{:S(2)}) copy-start(f32[2,8,512]{2,1,0:T(8,128)} %get-tuple-element.209) | copy-start | bytes 98308 | tf_op jit(solution)/shard_map/while
  207.6 4.6 %copy-start.6 = (f32[2,8,512]{2,1,0:T(8,128)S(1)}, f32[2,8,512]{2,1,0:T(8,128)}, u32[]{:S(2)}) copy-start(f32[2,8,512]{2,1,0:T(8,128)} %get-tuple-element.210) | copy-start | bytes 98308 | tf_op jit(solution)/shard_map/while
  212.3 9.5 %copy-start.7 = (f32[2,8,512]{2,1,0:T(8,128)}, f32[2,8,512]{2,1,0:T(8,128)S(1)}, u32[]{:S(2)}) copy-start(f32[2,8,512]{2,1,0:T(8,128)S(1)} %get-tuple-element.223) | copy-start | bytes 98308 | tf_op jit(solution)/shard_map/while
  224.4 4.2 %copy-start.1 = (f32[2,8,512]{2,1,0:T(8,128)S(1)}, f32[2,8,512]{2,1,0:T(8,128)}, u32[]{:S(2)}) copy-start(f32[2,8,512]{2,1,0:T(8,128)} %get-tuple-element.209) | copy-start | bytes 98308 | tf_op jit(solution)/shard_map/while
  228.7 4.6 %copy-start.6 = (f32[2,8,512]{2,1,0:T(8,128)S(1)}, f32[2,8,512]{2,1,0:T(8,128)}, u32[]{:S(2)}) copy-start(f32[2,8,512]{2,1,0:T(8,128)} %get-tuple-element.210) | copy-start | bytes 98308 | tf_op jit(solution)/shard_map/while
  233.4 9.5 %copy-start.7 = (f32[2,8,512]{2,1,0:T(8,128)}, f32[2,8,512]{2,1,0:T(8,128)S(1)}, u32[]{:S(2)}) copy-start(f32[2,8,512]{2,1,0:T(8,128)S(1)} %get-tuple-element.223) | copy-start | bytes 98308 | tf_op jit(solution)/shard_map/while
  245.5 4.2 %copy-start.1 = (f32[2,8,512]{2,1,0:T(8,128)S(1)}, f32[2,8,512]{2,1,0:T(8,128)}, u32[]{:S(2)}) copy-start(f32[2,8,512]{2,1,0:T(8,128)} %get-tuple-element.209) | copy-start | bytes 98308 | tf_op jit(solution)/shard_map/while
  249.7 4.6 %copy-start.6 = (f32[2,8,512]{2,1,0:T(8,128)S(1)}, f32[2,8,512]{2,1,0:T(8,128)}, u32[]{:S(2)}) copy-start(f32[2,8,512]{2,1,0:T(8,128)} %get-tuple-element.210) | copy-start | bytes 98308 | tf_op jit(solution)/shard_map/while
  254.4 9.5 %copy-start.7 = (f32[2,8,512]{2,1,0:T(8,128)}, f32[2,8,512]{2,1,0:T(8,128)S(1)}, u32[]{:S(2)}) copy-start(f32[2,8,512]{2,1,0:T(8,128)S(1)} %get-tuple-element.223) | copy-start | bytes 98308 | tf_op jit(solution)/shard_map/while
  266.5 4.2 %copy-start.1 = (f32[2,8,512]{2,1,0:T(8,128)S(1)}, f32[2,8,512]{2,1,0:T(8,128)}, u32[]{:S(2)}) copy-start(f32[2,8,512]{2,1,0:T(8,128)} %get-tuple-element.209) | copy-start | bytes 98308 | tf_op jit(solution)/shard_map/while
  270.8 4.6 %copy-start.6 = (f32[2,8,512]{2,1,0:T(8,128)S(1)}, f32[2,8,512]{2,1,0:T(8,128)}, u32[]{:S(2)}) copy-start(f32[2,8,512]{2,1,0:T(8,128)} %get-tuple-element.210) | copy-start | bytes 98308 | tf_op jit(solution)/shard_map/while
  275.5 9.5 %copy-start.7 = (f32[2,8,512]{2,1,0:T(8,128)}, f32[2,8,512]{2,1,0:T(8,128)S(1)}, u32[]{:S(2)}) copy-start(f32[2,8,512]{2,1,0:T(8,128)S(1)} %get-tuple-element.223) | copy-start | bytes 98308 | tf_op jit(solution)/shard_map/while
  285.6 3.9 %copy-start.2 = (f32[2,8,512]{2,1,0:T(8,128)S(1)}, f32[2,8,512]{2,1,0:T(8,128)}, u32[]{:S(2)}) copy-start(f32[2,8,512]{2,1,0:T(8,128)} %get-tuple-element.57) | copy-start | bytes 98308
  285.6 9.6 %copy-start.3 = (pred[512,512]{0,1:T(8,128)(4,1)S(1)}, pred[512,512]{0,1:T(8,128)(4,1)}, u32[]{:S(2)}) copy-start(pred[512,512]{0,1:T(8,128)(4,1)} %iota_compare_fusion) | copy-start | bytes 786436
  289.5 5.7 %copy-start = (f32[2,512,512,8]{2,1,3,0:T(8,128)}, f32[2,512,512,8]{2,1,3,0:T(8,128)S(1)}, u32[]{:S(2)}) copy-start(f32[2,512,512,8]{2,1,3,0:T(8,128)S(1)} %get-tuple-element.124) | copy-start | bytes 50331652
  295.2 4.0 %copy-start.8 = (f32[2,8,512]{2,1,0:T(8,128)S(1)}, f32[2,8,512]{2,1,0:T(8,128)}, u32[]{:S(2)}) copy-start(f32[2,8,512]{2,1,0:T(8,128)} %get-tuple-element.58) | copy-start | bytes 98308
  295.2 4.1 %copy-start.4 = (f32[2,8,512,128]{3,2,1,0:T(8,128)S(1)}, f32[2,8,512,128]{3,2,1,0:T(8,128)}, u32[]{:S(2)}) copy-start(f32[2,8,512,128]{3,2,1,0:T(8,128)} %get-tuple-element.56) | copy-start | bytes 12582916
  295.2 4.1 %copy-start.9 = (bf16[512,2,128,1]{2,1,0,3:T(2,128)(2,1)S(1)}, bf16[512,2,128,1]{2,1,0,3:T(2,128)(2,1)}, u32[]{:S(2)}) copy-start(bf16[512,2,128,1]{2,1,0,3:T(2,128)(2,1)} %fusion.22) | copy-start | bytes 786436
where the time goes:
time: 339 us; the launch traced here: 338 us
  waiting for transfers between devices  108 us (32%)
  matrix products  69.4 us (20%)
  blocking collectives  61.8 us (18%)
  other arithmetic  41.1 us (12%)
  local copies, waits for them, and re-layouts  30.6 us (9%)
  starting transfers between devices  23.2 us (7%)
  between operations  3.5 us (1%)
    all_to_all x1, waiting for transfers between devices, body(): lax.all_to_all(split_rows(q_new, slot_count), 'seq', split_axis=0, concat...  49 us
    dot_general x5, matrix products, attend_block(): jnp.einsum('kgqt,tkd->kgqd', weight.astype(jnp.bfloat16), value_rows, pre...  48.6 us
    all_to_all x1, waiting for transfers between devices, body(): lax.all_to_all(picked[0], 'seq', split_axis=0, concat_axis=0, tiled=True)  40.2 us
    all_to_all x1, blocking collectives, body(): lax.all_to_all(split_rows(k_new, slot_count), 'seq', split_axis=0, concat...  23.9 us
    reduce_sum x5, other arithmetic, attend_block(): new_sum = running_sum * factor + jnp.sum(weight, axis=-1)  22.5 us
    dot_general x5, matrix products, attend_block(): jnp.einsum('qkgd,tkd->kgqt', queries, key_rows, preferred_element_type=jn...  20.8 us
    all_to_all x1, blocking collectives, body(): lax.all_to_all(split_rows(v_new, slot_count), 'seq', split_axis=0, concat...  17.9 us
    psum x1, blocking collectives, body(): squares = lax.psum(jnp.sum(last_row * last_row), 'tp')  10.7 us
  transfers between devices with their start and end apart: 4, of which 4 were waited for; matrix products, arithmetic and copies ran while one was open for 5% of the time, Pallas kernels for 0%

commit v1 on v0

v1 whole, which is shorter than its diff:
```python
import functools
import math

import jax
import jax.numpy as jnp
from jax import lax
from jax.experimental import pallas as pl
from jax.experimental.pallas import tpu as pltpu
from jax.sharding import PartitionSpec as P

HEAD = 128
MESH = pl.DeviceIdType.MESH

theta_base = 1000000.0
norm_epsilon = 1e-06
scale = HEAD**-0.5
exp2_scale = scale * math.log2(math.e)
low_score = -3.0e38


def tables(length, rows):
    half_dim = HEAD // 2
    positions = length + jnp.arange(rows, dtype=jnp.int32)
    frequency = theta_base ** (-2.0 * jnp.arange(half_dim, dtype=jnp.float32) / HEAD)
    angles = positions.astype(jnp.float32)[:, None] * frequency[None, :]
    cosine, sine = jnp.cos(angles), jnp.sin(angles)
    return (
        jnp.concatenate([cosine, cosine], axis=1),
        jnp.concatenate([-sine, sine], axis=1),
    )


def rope(x, cosine, sine):
    return x * cosine + pltpu.roll(x, HEAD // 2, 1) * sine


def attention_kernel(
    length_ref, tok, q_bias, k_bias, v_bias, cache_k, cache_v, cosine, sine,
    out, new_keys, new_values, stats,
    keys, values, s_a, s_b, m_a, m_b,
):
    rows = tok.shape[1]
    kv_count = tok.shape[0]
    cached = cache_k.shape[0]
    group = tok.shape[2] // HEAD - 2
    half = 256
    halves = rows // half
    length = length_ref[0]

    stats[...] = jnp.zeros_like(stats)
    stats[1:2, :] = jnp.full((1, HEAD), low_score, jnp.float32)
    causal = lax.broadcasted_iota(jnp.int32, (half, half), 1) <= lax.broadcasted_iota(
        jnp.int32, (half, half), 0
    )

    def prepare(kv):
        at = slice(kv * HEAD, (kv + 1) * HEAD)
        valid = lax.broadcasted_iota(jnp.int32, (cached, HEAD), 0) < length
        keys[:cached, :] = jnp.where(valid, cache_k[:, at], cache_k[0:1, at])
        values[:cached, :HEAD] = jnp.where(valid, cache_v[:, at], jnp.bfloat16(0))
        values[:cached, HEAD:] = jnp.where(valid, jnp.bfloat16(1), jnp.bfloat16(0))
        fresh = tok[kv, :, group * HEAD : (group + 1) * HEAD].astype(jnp.float32)
        fresh = fresh + k_bias[0:1, at].astype(jnp.float32)
        fresh = rope(fresh, cosine[...], sine[...]).astype(jnp.bfloat16)
        keys[cached:, :] = fresh
        new_keys[:, at] = fresh
        fresh = tok[kv, :, (group + 1) * HEAD :].astype(jnp.float32)
        fresh = (fresh + v_bias[0:1, at].astype(jnp.float32)).astype(jnp.bfloat16)
        values[cached:, :HEAD] = fresh
        values[cached:, HEAD:] = jnp.ones((rows, HEAD), jnp.bfloat16)
        new_values[:, at] = fresh

    def key_blocks(part):
        blocks = [(first, False) for first in range(0, cached, half)]
        blocks += [(cached + half * i, i == part) for i in range(part + 1)]
        return blocks

    def score(kv, head, s_ref, m_ref):
        at = pl.ds(pl.multiple_of(head * HEAD, HEAD), HEAD)
        bias_at = pl.ds(pl.multiple_of((kv * group + head) * HEAD, HEAD), HEAD)
        bias = q_bias[0:1, bias_at].astype(jnp.float32)
        for part in range(halves):
            here = slice(part * half, (part + 1) * half)
            x = tok[kv, here, at].astype(jnp.float32) + bias
            query = rope(x, cosine[here, :], sine[here, :]).astype(jnp.bfloat16)
            largest = None
            for first, masked in key_blocks(part):
                s = lax.dot_general(
                    query, keys[first : first + half, :],
                    (((1,), (1,)), ((), ())), preferred_element_type=jnp.float32,
                )
                if masked:
                    s = jnp.where(causal, s, low_score)
                s_ref[here, first : first + half] = s
                local = jnp.maximum(s[:, :HEAD], s[:, HEAD:])
                largest = local if largest is None else jnp.maximum(largest, local)
            m_ref[here, :] = jnp.broadcast_to(
                jnp.max(largest, axis=1, keepdims=True), (half, HEAD)
            )

    def mix(kv, head, s_ref, m_ref):
        out_at = pl.ds(pl.multiple_of((kv * group + head) * HEAD, HEAD), HEAD)
        for part in range(halves):
            here = slice(part * half, (part + 1) * half)
            m = m_ref[here, :]
            m2 = jnp.concatenate([m, m], axis=1)
            total = None
            for first, masked in key_blocks(part):
                w = jnp.exp2((s_ref[here, first : first + half] - m2) * exp2_scale)
                term = jnp.dot(
                    w.astype(jnp.bfloat16), values[first : first + half, :],
                    preferred_element_type=jnp.float32,
                )
                total = term if total is None else total + term
            mixture = total[:, :HEAD] / total[:, HEAD:]
            out[here, out_at] = mixture.astype(jnp.bfloat16)
            if part == halves - 1:
                last = mixture[half - 1 : half, :]
                stats[0:1, :] = stats[0:1, :] + last * last
                stats[1:2, :] = jnp.maximum(stats[1:2, :], m[half - 1 : half, :] * scale)

    for kv in range(kv_count):
        prepare(kv)
        score(kv, 0, s_a, m_a)

        @pl.loop(0, group // 2 - 1)
        def _(i):
            score(kv, 2 * i + 1, s_b, m_b)
            mix(kv, 2 * i, s_a, m_a)
            score(kv, 2 * i + 2, s_a, m_a)
            mix(kv, 2 * i + 1, s_b, m_b)

        score(kv, group - 1, s_b, m_b)
        mix(kv, group - 2, s_a, m_a)
        mix(kv, group - 1, s_b, m_b)


def attend(length, tok, q_bias, k_bias, v_bias, cache_k, cache_v, cosine, sine):
    kv_count, rows, _ = tok.shape
    cached = cache_k.shape[0]
    vmem = pl.BlockSpec(memory_space=pltpu.VMEM)
    return pl.pallas_call(
        attention_kernel,
        out_shape=(
            jax.ShapeDtypeStruct((rows, q_bias.shape[0]), jnp.bfloat16),
            jax.ShapeDtypeStruct((rows, kv_count * HEAD), jnp.bfloat16),
            jax.ShapeDtypeStruct((rows, kv_count * HEAD), jnp.bfloat16),
            jax.ShapeDtypeStruct((8, HEAD), jnp.float32),
        ),
        in_specs=[pl.BlockSpec(memory_space=pltpu.SMEM)] + [vmem] * 8,
        out_specs=[vmem] * 4,
        scratch_shapes=[
            pltpu.VMEM((cached + rows, HEAD), jnp.bfloat16),
            pltpu.VMEM((cached + rows, 2 * HEAD), jnp.bfloat16),
            pltpu.VMEM((rows, cached + rows), jnp.float32),
            pltpu.VMEM((rows, cached + rows), jnp.float32),
            pltpu.VMEM((rows, HEAD), jnp.float32),
            pltpu.VMEM((rows, HEAD), jnp.float32),
        ],
        compiler_params=pltpu.CompilerParams(vmem_limit_bytes=48 << 20),
        name="attention",
    )(
        length.reshape(1), tok, q_bias.reshape(1, -1), k_bias.reshape(1, -1),
        v_bias.reshape(1, -1), cache_k, cache_v, cosine, sine,
    )


def stats_kernel(n, width, own, out, inbox, send_sems, recv_sems):
    me = lax.axis_index("tp")
    barrier = pltpu.get_barrier_semaphore()
    for step in range(1, n):
        pl.semaphore_signal(barrier, inc=1, device_id={"tp": lax.rem(me + step, n)}, device_id_type=MESH)
    pl.semaphore_wait(barrier, n - 1)
    copies = []
    for step in range(1, n):
        copy = pltpu.make_async_remote_copy(
            src_ref=own, dst_ref=inbox.at[step - 1],
            send_sem=send_sems.at[step - 1], recv_sem=recv_sems.at[step - 1],
            device_id={"tp": lax.rem(me + step, n)}, device_id_type=MESH,
        )
        copy.start()
        copies.append(copy)
    for copy in copies:
        copy.wait()
    squares, top = own[0:1, :], own[1:2, :]
    for step in range(1, n):
        squares = squares + inbox[step - 1, 0:1, :]
        top = jnp.maximum(top, inbox[step - 1, 1:2, :])
    norm = jnp.sqrt(jnp.sum(squares, axis=1, keepdims=True) / width + norm_epsilon)
    top = jnp.max(top, axis=1, keepdims=True)
    out[0:1, :] = jnp.broadcast_to(norm, (1, HEAD))
    out[1:2, :] = jnp.broadcast_to(top, (1, HEAD))


def reduce_stats(stats, width):
    n = lax.axis_size("tp")
    vmem = pl.BlockSpec(memory_space=pltpu.VMEM)
    out = pl.pallas_call(
        functools.partial(stats_kernel, n, width),
        out_shape=jax.ShapeDtypeStruct((8, HEAD), jnp.float32),
        in_specs=[vmem],
        out_specs=vmem,
        scratch_shapes=[
            pltpu.VMEM((n - 1, 8, HEAD), jnp.float32),
            pltpu.SemaphoreType.DMA((n - 1,)),
            pltpu.SemaphoreType.DMA((n - 1,)),
        ],
        compiler_params=pltpu.CompilerParams(collective_id=1, has_side_effects=True),
        name="stats",
    )(stats)
    return out[0, 0:1], out[1, 0:1]


def split_kv(q, k, v):
    kv_count = k.shape[1] // HEAD
    wide = q.shape[1] // kv_count
    return jnp.stack(
        [
            jnp.concatenate(
                [
                    q[:, i * wide : (i + 1) * wide],
                    k[:, i * HEAD : (i + 1) * HEAD],
                    v[:, i * HEAD : (i + 1) * HEAD],
                ],
                axis=1,
            )
            for i in range(kv_count)
        ]
    )


def exchange(tok, deal):
    slots = lax.axis_size("seq")
    slot_ids = jnp.arange(slots, dtype=jnp.int32)
    inverse = jnp.sum(jnp.where(deal[None, :] == slot_ids[:, None], slot_ids[None, :], 0), axis=1)
    flat = tok.reshape(slots, -1, tok.shape[2])
    spread = lax.all_to_all(flat, "seq", split_axis=0, concat_axis=0, tiled=True)
    picked = jnp.take(spread, inverse, axis=0)
    settled = lax.all_to_all(picked, "seq", split_axis=0, concat_axis=0, tiled=True)
    return settled.reshape(tok.shape)


def body(q_new, k_new, v_new, q_bias, k_bias, v_bias, cache_k, cache_v, deal, cache_len):
    rows = q_new.shape[0]
    length = cache_len[lax.axis_index("seq")]
    cosine, sine = tables(length, rows)
    tok = exchange(split_kv(q_new, k_new, v_new), deal)
    attn_out, new_keys, new_values, stats = attend(
        length, tok, q_bias, k_bias, v_bias, cache_k, cache_v, cosine, sine
    )
    last_norm, top_logit = reduce_stats(stats, q_new.shape[1] * lax.axis_size("tp"))
    return attn_out, new_keys, new_values, last_norm, top_logit


def solution(mesh):
    return jax.shard_map(
        body,
        mesh=mesh,
        in_specs=(
            P("seq", "tp"), P("seq", "tp"), P("seq", "tp"), P("tp"), P("tp"), P("tp"),
            P("seq", "tp"), P("seq", "tp"), P(), P(),
        ),
        out_specs=(P("seq", "tp"), P("seq", "tp"), P("seq", "tp"), P("seq"), P("seq")),
        check_vma=False,
    )
```

time: 339 us -> 192 us (0.57)
  matrix products: 69.4 us -> 0 us
  blocking collectives: 61.8 us -> 0 us
  other arithmetic: 41.1 us -> 7.49 us
  Pallas kernels: 0 us -> 33.3 us
  local copies, waits for them, and re-layouts: 30.6 us -> 8.96 us
  waiting for transfers between devices: 108 us -> 122 us
  starting transfers between devices: 23.2 us -> 17.7 us
    dot_general x10 -> x0, matrix products: 69.4 us -> none  [the longest x5 48.6 us: attend_block(): jnp.einsum('kgqt,tkd->kgqd', weight.astype(jnp.bfloat16), value_rows, pre...]
    all_to_all x2 -> x0, blocking collectives: 41.8 us -> none  [the longest x1 23.9 us: body(): lax.all_to_all(split_rows(k_new, slot_count), 'seq', split_axis=0, concat...]
    pallas_call x0 -> x2, Pallas kernels: none -> 33.3 us  [the longest x1 26.7 us: attend(): pl.pallas_call(attention_kernel, out_shape=(jax.ShapeDtypeStruct((rows, q...]
    reduce_sum x7 -> x1, other arithmetic: 23.2 us -> 0.11 us  [exchange(): jnp.sum(jnp.where(deal[None, :] == slot_ids[:, None], slot_ids[None, :],...]
    all_to_all x4 -> x2, waiting for transfers between devices: 108 us -> 122 us  [the longest x1 62.4 us: exchange(): lax.all_to_all(flat, 'seq', split_axis=0, concat_axis=0, tiled=True)]
    psum x1 -> x0, blocking collectives: 10.7 us -> none  [body(): squares = lax.psum(jnp.sum(last_row * last_row), 'tp')]
    pmax x1 -> x0, blocking collectives: 9.22 us -> none  [body(): top_value = lax.pmax(jnp.max(carry_state[0][:, :, row_count - 1]), 'tp')]
    unnamed x27 -> x20, local copies, waits for them, and re-layouts: 9.07 us -> 3.07 us
  transfers between devices with their start and end apart: 4 -> 2, of which waited for: 4 -> 2; matrix products, arithmetic and copies ran while one was open for 5% -> 1% of each run, Pallas kernels for 0% -> 0%
where the time goes in v1:
time: 192 us; the launch traced here: 191 us
  waiting for transfers between devices  122 us (64%)
  Pallas kernels  33.3 us (17%)
  starting transfers between devices  17.7 us (9%)
  local copies, waits for them, and re-layouts  8.96 us (5%)
  other arithmetic  7.49 us (4%)
    all_to_all x1, waiting for transfers between devices, exchange(): lax.all_to_all(flat, 'seq', split_axis=0, concat_axis=0, tiled=True)  62.4 us
    all_to_all x1, waiting for transfers between devices, exchange(): lax.all_to_all(picked, 'seq', split_axis=0, concat_axis=0, tiled=True)  60 us
    pallas_call x1, Pallas kernels, attend(): pl.pallas_call(attention_kernel, out_shape=(jax.ShapeDtypeStruct((rows, q...  26.7 us
    all_to_all x1, starting transfers between devices, exchange(): lax.all_to_all(flat, 'seq', split_axis=0, concat_axis=0, tiled=True)  12.1 us
    pallas_call x1, Pallas kernels, reduce_stats(): pl.pallas_call(functools.partial(stats_kernel, n, width), out_shape=jax.S...  6.55 us
    all_to_all x1, starting transfers between devices, exchange(): lax.all_to_all(picked, 'seq', split_axis=0, concat_axis=0, tiled=True)  5.57 us
  transfers between devices with their start and end apart: 2, of which 2 were waited for; matrix products, arithmetic and copies ran while one was open for 1% of the time, Pallas kernels for 0%

profile of v1, /device:TPU:18, one launch (start us, length us, event | category | flops | bytes accessed | tf_op | source)
XLA Modules:
  0.0 190.5 jit_solution(9995999827582163404)
XLA Ops:
  0.6 0.0 copy-start.3
  0.6 0.0 copy-start.4
  0.7 1.8 fusion.2
  2.4 0.0 copy-done.3
  2.5 0.0 copy-done.4
  2.5 0.2 maximum_bitcast_fusion
  2.8 1.7 pad_maximum_fusion
  4.5 0.0 copy-start.6
  4.5 12.1 %all-to-all-start = ((bf16[64,16,1280]{2,1,0:T(8,128)(2,1)}), bf16[64,16,1280]{2,1,0:T(8,128)(2,1)S(1)}, u32[]{:S(2)}, u32[]{:S(2)}) async-start(bf16[64,16,1280]{2,1,0:T(8,128)(2,1)} %bitcast.14), calls=%async_computation | async-start | bytes 5242880 | tf_op jit(solution)/shard_map/all_to_all | solution.py:237
  16.6 0.0 copy-done.6
  16.6 0.1 select_reduce_fusion
  16.8 62.4 %all-to-all-done = bf16[64,16,1280]{2,1,0:T(8,128)(2,1)S(1)} async-done(((bf16[64,16,1280]{2,1,0:T(8,128)(2,1)}), bf16[64,16,1280]{2,1,0:T(8,128)(2,1)S(1)}, u32[]{:S(2)}, u32[]{:S(2)}) %all-to-all-start) | async-done | bytes 2621472 | tf_op jit(solution)/shard_map/all_to_all | solution.py:237
  79.1 2.2 %gather_fusion = bf16[64,16,1280]{2,1,0:T(8,128)(2,1)} fusion(bf16[64,16,1280]{2,1,0:T(8,128)(2,1)S(1)} %all-to-all-done, s32[1024]{0:T(1024)S(1)} %pad_clamp_fusion), kind=kCustom, calls=%fused_computation | custom fusion | bytes 5243136 | tf_op jit(solution)/shard_map/jit(_take)/gather | solution.py:238
  81.3 3.5 %broadcast_select_fusion = bf16[64,16,1280]{2,1,0:T(8,128)(2,1)} fusion(bf16[64,16,1280]{2,1,0:T(8,128)(2,1)} %gather_fusion, pred[64]{0:T(512)(128)(4,1)S(1)} %compare_and_fusion), kind=kLoop, calls=%fused_computation.2 | loop fusion | flops 1310720 | bytes 5242944 | tf_op jit(solution)/shard_map/jit(_take)/select_n | solution.py:238
  84.9 0.0 copy-start.5
  84.9 0.0 copy-start.7
  84.9 5.6 %all-to-all-start.1 = ((bf16[64,16,1280]{2,1,0:T(8,128)(2,1)}), bf16[64,16,1280]{2,1,0:T(8,128)(2,1)S(1)}, u32[]{:S(2)}, u32[]{:S(2)}) async-start(bf16[64,16,1280]{2,1,0:T(8,128)(2,1)} %broadcast_select_fusion), calls=%async_computation.1 | async-start | bytes 5242880 | tf_op jit(solution)/shard_map/all_to_all | solution.py:239
  90.5 0.0 copy-done.5
  90.5 0.0 copy-done.7
  90.5 0.0 copy-done.8
  90.5 0.0 copy-done.9
  90.5 0.6 dynamic_slice.3.length_ref
  91.1 0.7 add_convert_fusion
  91.8 1.0 fusion
  92.8 0.2 pad_maximum_fusion.1
  93.0 60.0 %all-to-all-done.1 = bf16[64,16,1280]{2,1,0:T(8,128)(2,1)S(1)} async-done(((bf16[64,16,1280]{2,1,0:T(8,128)(2,1)}), bf16[64,16,1280]{2,1,0:T(8,128)(2,1)S(1)}, u32[]{:S(2)}, u32[]{:S(2)}) %all-to-all-start.1) | async-done | bytes 2621472 | tf_op jit(solution)/shard_map/all_to_all | solution.py:239
  153.0 1.2 copy-done
  154.2 1.2 copy-done.1
  155.4 26.7 %attention.1 = (bf16[512,2048]{1,0:T(8,128)(2,1)}, bf16[512,256]{1,0:T(8,128)(2,1)}, bf16[512,256]{1,0:T(8,128)(2,1)}, f32[8,128]{1,0:T(8,128)S(1)}) custom-call(s32[1]{0:T(128)} %dynamic_slice.3.length_ref, bf16[2,512,1280]{2,1,0:T(8,128)(2,1)S(1)} %bitcast.13, bf16[1,2048]{1,0:T(2,128)(2,1)S(1)} %reshape.56.q_bias, bf16[1,256]{1,0:T(2,128)(2,1)S(1)} %reshape.57.k_bias, ...), custom_call_target="tpu_custom_call" | custom-call | tf_op jit(solution)/shard_map/attention/pallas_call | solution.py:142
  182.1 0.6 copy-done.2
  182.7 6.6 %stats.1 = f32[8,128]{1,0:T(8,128)} custom-call(f32[8,128]{1,0:T(8,128)} %copy-done.2), custom_call_target="tpu_custom_call" | custom-call | tf_op jit(solution)/shard_map/stats/pallas_call | solution.py:198
  189.3 1.3 fusion.5
  (14 shorter events, 0.1 us)
Async XLA Ops:
  0.6 1.8 copy-start.3
  0.6 1.8 copy-start.4
  4.5 12.1 %copy-start.6 = (s32[64]{0:T(128)S(1)}, s32[64]{0:T(128)}, u32[]{:S(2)}) copy-start(s32[64]{0:T(128)} %param.18) | copy-start | bytes 772
  4.5 74.6 %all-to-all-start = ((bf16[64,16,1280]{2,1,0:T(8,128)(2,1)}), bf16[64,16,1280]{2,1,0:T(8,128)(2,1)S(1)}, u32[]{:S(2)}, u32[]{:S(2)}) async-start(bf16[64,16,1280]{2,1,0:T(8,128)(2,1)} %bitcast.14), calls=%async_computation | async-start | bytes 5242880 | tf_op jit(solution)/shard_map/all_to_all | solution.py:237
  84.9 5.6 %copy-start.5 = (bf16[2048]{0:T(1024)(128)(2,1)S(1)}, bf16[2048]{0:T(1024)(128)(2,1)}, u32[]{:S(2)}) copy-start(bf16[2048]{0:T(1024)(128)(2,1)} %param.13) | copy-start | bytes 12292
  84.9 5.6 %copy-start.7 = (bf16[256]{0:T(256)(128)(2,1)S(1)}, bf16[256]{0:T(256)(128)(2,1)}, u32[]{:S(2)}) copy-start(bf16[256]{0:T(256)(128)(2,1)} %param.14) | copy-start | bytes 1540
  84.9 5.6 %copy-start.8 = (bf16[256]{0:T(256)(128)(2,1)S(1)}, bf16[256]{0:T(256)(128)(2,1)}, u32[]{:S(2)}) copy-start(bf16[256]{0:T(256)(128)(2,1)} %param.15) | copy-start | bytes 1540
  84.9 5.7 %copy-start.9 = (s32[64]{0:T(128)S(1)}, s32[64]{0:T(128)}, u32[]{:S(2)}) copy-start(s32[64]{0:T(128)} %param.19) | copy-start | bytes 772
  84.9 68.1 %all-to-all-start.1 = ((bf16[64,16,1280]{2,1,0:T(8,128)(2,1)}), bf16[64,16,1280]{2,1,0:T(8,128)(2,1)S(1)}, u32[]{:S(2)}, u32[]{:S(2)}) async-start(bf16[64,16,1280]{2,1,0:T(8,128)(2,1)} %broadcast_select_fusion), calls=%async_computation.1 | async-start | bytes 5242880 | tf_op jit(solution)/shard_map/all_to_all | solution.py:239
  153.0 1.2 copy-start
  154.2 1.2 copy-start.1
  182.1 0.6 copy-start.2

commit v2 on v1

--- a/solution.py
+++ b/solution.py
@@ -35,10 +35,9 @@
 
 
 def attention_kernel(
-    length_ref, tok, q_bias, k_bias, v_bias, cache_k, cache_v, cosine, sine,
-    out, new_keys, new_values, stats,
-    keys, values, s_a, s_b, m_a, m_b,
+    carried, length_ref, tok, q_bias, k_bias, v_bias, cache_k, cache_v, cosine, sine, *refs
 ):
+    out, new_keys, new_values, stats, keys, values, s_a, s_b, m_a, m_b = refs[carried:]
     rows = tok.shape[1]
     kv_count = tok.shape[0]
     cached = cache_k.shape[0]
@@ -135,20 +134,33 @@
         mix(kv, group - 1, s_b, m_b)
 
 
-def attend(length, tok, q_bias, k_bias, v_bias, cache_k, cache_v, cosine, sine):
-    kv_count, rows, _ = tok.shape
+def attend(kv, kv_count, carried, length, tok, q_bias, k_bias, v_bias, cache_k, cache_v, cosine, sine):
+    _, rows, _ = tok.shape
     cached = cache_k.shape[0]
-    vmem = pl.BlockSpec(memory_space=pltpu.VMEM)
+    wide = q_bias.shape[0] // kv_count
+    whole = lambda shape: pl.BlockSpec(shape, lambda i: (0,) * len(shape))
+    columns = lambda count, width: pl.BlockSpec((count, width), lambda i: (0, kv))
+    out_shape = (
+        jax.ShapeDtypeStruct((rows, kv_count * wide), jnp.bfloat16),
+        jax.ShapeDtypeStruct((rows, kv_count * HEAD), jnp.bfloat16),
+        jax.ShapeDtypeStruct((rows, kv_count * HEAD), jnp.bfloat16),
+    )
+    operands = 9
+    flops = 2 * rows * (cached + rows) * 3 * wide
     return pl.pallas_call(
-        attention_kernel,
-        out_shape=(
-            jax.ShapeDtypeStruct((rows, q_bias.shape[0]), jnp.bfloat16),
-            jax.ShapeDtypeStruct((rows, kv_count * HEAD), jnp.bfloat16),
-            jax.ShapeDtypeStruct((rows, kv_count * HEAD), jnp.bfloat16),
-            jax.ShapeDtypeStruct((8, HEAD), jnp.float32),
-        ),
-        in_specs=[pl.BlockSpec(memory_space=pltpu.SMEM)] + [vmem] * 8,
-        out_specs=[vmem] * 4,
+        functools.partial(attention_kernel, len(carried)),
+        grid=(1,),
+        out_shape=out_shape + (jax.ShapeDtypeStruct((8, HEAD), jnp.float32),),
+        in_specs=[
+            pl.BlockSpec(memory_space=pltpu.SMEM),
+            whole(tok.shape),
+            columns(1, wide), columns(1, HEAD), columns(1, HEAD),
+            columns(cached, HEAD), columns(cached, HEAD),
+            whole(cosine.shape), whole(sine.shape),
+        ] + [pl.BlockSpec(memory_space=pl.ANY)] * len(carried),
+        out_specs=[
+            columns(rows, wide), columns(rows, HEAD), columns(rows, HEAD), whole((8, HEAD)),
+        ],
         scratch_shapes=[
             pltpu.VMEM((cached + rows, HEAD), jnp.bfloat16),
             pltpu.VMEM((cached + rows, 2 * HEAD), jnp.bfloat16),
@@ -157,11 +169,15 @@
             pltpu.VMEM((rows, HEAD), jnp.float32),
             pltpu.VMEM((rows, HEAD), jnp.float32),
         ],
+        input_output_aliases={operands + i: i for i in range(len(carried))},
         compiler_params=pltpu.CompilerParams(vmem_limit_bytes=48 << 20),
+        cost_estimate=pl.CostEstimate(
+            flops=flops, bytes_accessed=8 << 20, transcendentals=rows * (cached + rows) * (wide // HEAD)
+        ),
         name="attention",
     )(
         length.reshape(1), tok, q_bias.reshape(1, -1), k_bias.reshape(1, -1),
-        v_bias.reshape(1, -1), cache_k, cache_v, cosine, sine,
+        v_bias.reshape(1, -1), cache_k, cache_v, cosine, sine, *carried,
     )
 
 
@@ -192,8 +208,14 @@
     out[1:2, :] = jnp.broadcast_to(top, (1, HEAD))
 
 
-def reduce_stats(stats, width):
+def reduce_stats(parts, width):
     n = lax.axis_size("tp")
+    stats = jnp.concatenate(
+        [
+            functools.reduce(jnp.add, [part[0:1] for part in parts]),
+            functools.reduce(jnp.maximum, [part[1:] for part in parts]),
+        ]
+    )
     vmem = pl.BlockSpec(memory_space=pltpu.VMEM)
     out = pl.pallas_call(
         functools.partial(stats_kernel, n, width),
@@ -211,44 +233,42 @@
     return out[0, 0:1], out[1, 0:1]
 
 
-def split_kv(q, k, v):
-    kv_count = k.shape[1] // HEAD
-    wide = q.shape[1] // kv_count
-    return jnp.stack(
-        [
-            jnp.concatenate(
-                [
-                    q[:, i * wide : (i + 1) * wide],
-                    k[:, i * HEAD : (i + 1) * HEAD],
-                    v[:, i * HEAD : (i + 1) * HEAD],
-                ],
-                axis=1,
-            )
-            for i in range(kv_count)
-        ]
-    )
-
-
-def exchange(tok, deal):
+def packet(kv, q, k, v):
+    wide = q.shape[1] // (k.shape[1] // HEAD)
+    at = slice(kv * HEAD, (kv + 1) * HEAD)
+    return jnp.concatenate([q[:, kv * wide : (kv + 1) * wide], k[:, at], v[:, at]], axis=1)
+
+
+def spread(tok):
     slots = lax.axis_size("seq")
-    slot_ids = jnp.arange(slots, dtype=jnp.int32)
-    inverse = jnp.sum(jnp.where(deal[None, :] == slot_ids[:, None], slot_ids[None, :], 0), axis=1)
-    flat = tok.reshape(slots, -1, tok.shape[2])
-    spread = lax.all_to_all(flat, "seq", split_axis=0, concat_axis=0, tiled=True)
-    picked = jnp.take(spread, inverse, axis=0)
+    flat = tok.reshape(slots, -1, tok.shape[1])
+    return lax.all_to_all(flat, "seq", split_axis=0, concat_axis=0, tiled=True)
+
+
+def settle(scattered, inverse):
+    picked = jnp.take(scattered, inverse, axis=0, mode="clip")
     settled = lax.all_to_all(picked, "seq", split_axis=0, concat_axis=0, tiled=True)
-    return settled.reshape(tok.shape)
+    return settled.reshape(1, -1, scattered.shape[2])
 
 
 def body(q_new, k_new, v_new, q_bias, k_bias, v_bias, cache_k, cache_v, deal, cache_len):
     rows = q_new.shape[0]
+    kv_count = k_new.shape[1] // HEAD
     length = cache_len[lax.axis_index("seq")]
     cosine, sine = tables(length, rows)
-    tok = exchange(split_kv(q_new, k_new, v_new), deal)
-    attn_out, new_keys, new_values, stats = attend(
-        length, tok, q_bias, k_bias, v_bias, cache_k, cache_v, cosine, sine
-    )
-    last_norm, top_logit = reduce_stats(stats, q_new.shape[1] * lax.axis_size("tp"))
+    slot_ids = jnp.arange(lax.axis_size("seq"), dtype=jnp.int32)
+    inverse = jnp.sum(jnp.where(deal[None, :] == slot_ids[:, None], slot_ids[None, :], 0), axis=1)
+    scattered = [spread(packet(kv, q_new, k_new, v_new)) for kv in range(kv_count)]
+    arrived = [settle(part, inverse) for part in scattered]
+    carried, parts = (), []
+    for kv in range(kv_count):
+        *carried, part = attend(
+            kv, kv_count, carried, length, arrived[kv], q_bias, k_bias, v_bias,
+            cache_k, cache_v, cosine, sine,
+        )
+        parts.append(part)
+    attn_out, new_keys, new_values = carried
+    last_norm, top_logit = reduce_stats(parts, q_new.shape[1] * lax.axis_size("tp"))
     return attn_out, new_keys, new_values, last_norm, top_logit
 
 

time: 192 us -> 198 us (1.031)
  starting transfers between devices: 17.7 us -> 28.5 us
  waiting for transfers between devices: 122 us -> 115 us
  local copies, waits for them, and re-layouts: 8.96 us -> 12 us
  other arithmetic: 7.49 us -> 4.93 us
    all_to_all x2 -> x4, starting transfers between devices: 17.7 us -> 28.5 us  [the longest x2 17.5 us: spread(): return lax.all_to_all(flat, 'seq', split_axis=0, concat_axis=0, tiled=True)]
    all_to_all x2 -> x4, waiting for transfers between devices: 122 us -> 115 us  [the longest x2 65.8 us: spread(): return lax.all_to_all(flat, 'seq', split_axis=0, concat_axis=0, tiled=True)]
    select_n x2 -> x0, other arithmetic: 3.54 us -> none  [exchange(): picked = jnp.take(spread, inverse, axis=0)]
    gather x1 -> x2, local copies, waits for them, and re-layouts: 2.21 us -> 4.72 us  [settle(): picked = jnp.take(scattered, inverse, axis=0, mode='clip')]
    reshape x0 -> x2, other arithmetic: none -> 2.33 us  [spread(): flat = tok.reshape(slots, -1, tok.shape[1])]
    pallas_call x1 -> x2, Pallas kernels: 26.7 us -> 28.5 us  [attend(): pl.pallas_call(functools.partial(attention_kernel, len(carried)), grid=(1...]
  transfers between devices with their start and end apart: 2 -> 4, of which waited for: 2 -> 4; matrix products, arithmetic and copies ran while one was open for 1% -> 4% of each run, Pallas kernels for 0% -> 7%
where the time goes in v2:
time: 198 us; the launch traced here: 196 us
  waiting for transfers between devices  115 us (58%)
  Pallas kernels  35.1 us (18%)
  starting transfers between devices  28.5 us (14%)
  local copies, waits for them, and re-layouts  12 us (6%)
  other arithmetic  4.93 us (2%)
    all_to_all x2, waiting for transfers between devices, spread(): return lax.all_to_all(flat, 'seq', split_axis=0, concat_axis=0, tiled=True)  65.8 us
    all_to_all x2, waiting for transfers between devices, settle(): lax.all_to_all(picked, 'seq', split_axis=0, concat_axis=0, tiled=True)  49 us
    pallas_call x2, Pallas kernels, attend(): pl.pallas_call(functools.partial(attention_kernel, len(carried)), grid=(1...  28.5 us
    all_to_all x2, starting transfers between devices, spread(): return lax.all_to_all(flat, 'seq', split_axis=0, concat_axis=0, tiled=True)  17.5 us
    all_to_all x2, starting transfers between devices, settle(): lax.all_to_all(picked, 'seq', split_axis=0, concat_axis=0, tiled=True)  11 us
    pallas_call x1, Pallas kernels, reduce_stats(): pl.pallas_call(functools.partial(stats_kernel, n, width), out_shape=jax.S...  6.54 us
    gather x2, local copies, waits for them, and re-layouts, settle(): picked = jnp.take(scattered, inverse, axis=0, mode='clip')  4.72 us
  transfers between devices with their start and end apart: 4, of which 4 were waited for; matrix products, arithmetic and copies ran while one was open for 4% of the time, Pallas kernels for 7%

profile of v2, /device:TPU:18, one launch (start us, length us, event | category | flops | bytes accessed | tf_op | source)
XLA Modules:
  0.0 196.3 jit_solution(13964697056386113548)
XLA Ops:
  0.6 0.0 copy-start.6
  0.6 0.0 copy-start.5
  0.7 1.8 fusion.1
  2.4 0.1 fusion.2
  2.5 1.2 maximum_bitcast_fusion.1
  3.7 12.0 %all-to-all-start.2 = ((bf16[64,8,1280]{2,1,0:T(8,128)(2,1)}), bf16[64,8,1280]{2,1,0:T(8,128)(2,1)S(1)}, u32[]{:S(2)}, u32[]{:S(2)}) async-start(bf16[64,8,1280]{2,1,0:T(8,128)(2,1)} %maximum_bitcast_fusion.1), calls=%async_computation.2 | async-start | bytes 2621440 | tf_op jit(solution)/shard_map/all_to_all | solution.py:245
  15.7 1.2 maximum_bitcast_fusion
  16.9 33.3 %all-to-all-done.2 = bf16[64,8,1280]{2,1,0:T(8,128)(2,1)S(1)} async-done(((bf16[64,8,1280]{2,1,0:T(8,128)(2,1)}), bf16[64,8,1280]{2,1,0:T(8,128)(2,1)S(1)}, u32[]{:S(2)}, u32[]{:S(2)}) %all-to-all-start.2) | async-done | bytes 1310752 | tf_op jit(solution)/shard_map/all_to_all | solution.py:245
  50.1 5.5 %all-to-all-start = ((bf16[64,8,1280]{2,1,0:T(8,128)(2,1)}), bf16[64,8,1280]{2,1,0:T(8,128)(2,1)S(1)}, u32[]{:S(2)}, u32[]{:S(2)}) async-start(bf16[64,8,1280]{2,1,0:T(8,128)(2,1)} %maximum_bitcast_fusion), calls=%async_computation | async-start | bytes 2621440 | tf_op jit(solution)/shard_map/all_to_all | solution.py:245
  55.7 0.1 select_reduce_fusion
  55.8 1.7 gather_fusion.1
  57.5 32.6 %all-to-all-done = bf16[64,8,1280]{2,1,0:T(8,128)(2,1)S(1)} async-done(((bf16[64,8,1280]{2,1,0:T(8,128)(2,1)}), bf16[64,8,1280]{2,1,0:T(8,128)(2,1)S(1)}, u32[]{:S(2)}, u32[]{:S(2)}) %all-to-all-start) | async-done | bytes 1310752 | tf_op jit(solution)/shard_map/all_to_all | solution.py:245
  90.1 1.1 copy-done.4
  91.1 5.5 %all-to-all-start.3 = ((bf16[64,8,1280]{2,1,0:T(8,128)(2,1)}), bf16[64,8,1280]{2,1,0:T(8,128)(2,1)S(1)}, u32[]{:S(2)}, u32[]{:S(2)}) async-start(bf16[64,8,1280]{2,1,0:T(8,128)(2,1)} %gather_fusion.1), calls=%async_computation.3 | async-start | bytes 2621440 | tf_op jit(solution)/shard_map/all_to_all | solution.py:250
  96.6 3.0 %gather_fusion = bf16[64,8,1280]{2,1,0:T(8,128)(2,1)} fusion(bf16[64,8,1280]{2,1,0:T(8,128)(2,1)} %copy-done.4, s32[1024]{0:T(1024)S(1)} %pad_clamp_fusion), kind=kCustom, calls=%fused_computation | custom fusion | bytes 2621696 | tf_op jit(solution)/shard_map/jit(_take)/gather | solution.py:249
  99.7 31.4 %all-to-all-done.3 = bf16[64,8,1280]{2,1,0:T(8,128)(2,1)S(1)} async-done(((bf16[64,8,1280]{2,1,0:T(8,128)(2,1)}), bf16[64,8,1280]{2,1,0:T(8,128)(2,1)S(1)}, u32[]{:S(2)}, u32[]{:S(2)}) %all-to-all-start.3) | async-done | bytes 1310752 | tf_op jit(solution)/shard_map/all_to_all | solution.py:250
  131.1 5.5 %all-to-all-start.1 = ((bf16[64,8,1280]{2,1,0:T(8,128)(2,1)}), bf16[64,8,1280]{2,1,0:T(8,128)(2,1)S(1)}, u32[]{:S(2)}, u32[]{:S(2)}) async-start(bf16[64,8,1280]{2,1,0:T(8,128)(2,1)} %gather_fusion), calls=%async_computation.1 | async-start | bytes 2621440 | tf_op jit(solution)/shard_map/all_to_all | solution.py:250
  136.6 0.0 copy-done.10
  136.7 0.0 copy-start
  136.7 0.0 copy-start.2
  136.7 0.6 dynamic_slice.3.length_ref
  137.3 0.7 add_convert_fusion
  138.0 1.0 fusion
  139.0 0.2 pad_maximum_fusion
  139.2 14.2 %attention.2 = (bf16[512,2048]{1,0:T(8,128)(2,1)}, bf16[512,256]{1,0:T(8,128)(2,1)}, bf16[512,256]{1,0:T(8,128)(2,1)}, f32[8,128]{1,0:T(8,128)S(1)}) custom-call(s32[1]{0:T(128)} %dynamic_slice.3.length_ref, bf16[1,512,1280]{2,1,0:T(8,128)(2,1)S(1)} %bitcast.9, bf16[1,2048]{1,0:T(2,128)(2,1)S(1)} %reshape.47.q_bias, bf16[1,256]{1,0:T(2,128)(2,1)S(1)} %reshape.48.k_bias, ...), custom_call_target="tpu_custom_call" | custom-call | flops 8053063680 | bytes 8388608 | tf_op jit(solution)/shard_map/attention/pallas_call | solution.py:150
  153.4 17.6 %all-to-all-done.1 = bf16[64,8,1280]{2,1,0:T(8,128)(2,1)S(1)} async-done(((bf16[64,8,1280]{2,1,0:T(8,128)(2,1)}), bf16[64,8,1280]{2,1,0:T(8,128)(2,1)S(1)}, u32[]{:S(2)}, u32[]{:S(2)}) %all-to-all-start.1) | async-done | bytes 1310752 | tf_op jit(solution)/shard_map/all_to_all | solution.py:250
  171.0 1.2 copy-done.1
  172.2 1.2 copy-done.3
  173.5 14.4 %attention.3 = (bf16[512,2048]{1,0:T(8,128)(2,1)}, bf16[512,256]{1,0:T(8,128)(2,1)}, bf16[512,256]{1,0:T(8,128)(2,1)}, f32[8,128]{1,0:T(8,128)S(1)}) custom-call(s32[1]{0:T(128)} %dynamic_slice.3.length_ref, bf16[1,512,1280]{2,1,0:T(8,128)(2,1)S(1)} %bitcast.10, ...), custom_call_target="tpu_custom_call", output_to_operand_aliasing={{0}: (9, {}), {1}: (10, {}), {2}: (11, {})} | custom-call | flops 8053063680 | bytes 8388608 | tf_op jit(solution)/shard_map/attention/pallas_call | solution.py:150
  187.9 0.6 pad_maximum_fusion.2.own
  188.5 6.5 %stats.1 = f32[8,128]{1,0:T(8,128)} custom-call(f32[8,128]{1,0:T(8,128)} %pad_maximum_fusion.2.own), custom_call_target="tpu_custom_call" | custom-call | tf_op jit(solution)/shard_map/stats/pallas_call | solution.py:220
  195.0 1.3 fusion.4
  (23 shorter events, 0.1 us)
Async XLA Ops:
  0.6 1.8 copy-start.6
  0.6 1.8 copy-start.5
  3.7 46.4 %all-to-all-start.2 = ((bf16[64,8,1280]{2,1,0:T(8,128)(2,1)}), bf16[64,8,1280]{2,1,0:T(8,128)(2,1)S(1)}, u32[]{:S(2)}, u32[]{:S(2)}) async-start(bf16[64,8,1280]{2,1,0:T(8,128)(2,1)} %maximum_bitcast_fusion.1), calls=%async_computation.2 | async-start | bytes 2621440 | tf_op jit(solution)/shard_map/all_to_all | solution.py:245
  16.9 38.8 %copy-start.8 = (s32[64]{0:T(128)S(1)}, s32[64]{0:T(128)}, u32[]{:S(2)}) copy-start(s32[64]{0:T(128)} %param.18) | copy-start | bytes 772
  50.1 39.9 %all-to-all-start = ((bf16[64,8,1280]{2,1,0:T(8,128)(2,1)}), bf16[64,8,1280]{2,1,0:T(8,128)(2,1)S(1)}, u32[]{:S(2)}, u32[]{:S(2)}) async-start(bf16[64,8,1280]{2,1,0:T(8,128)(2,1)} %maximum_bitcast_fusion), calls=%async_computation | async-start | bytes 2621440 | tf_op jit(solution)/shard_map/all_to_all | solution.py:245
  90.1 1.1 copy-start.4
  91.1 39.9 %all-to-all-start.3 = ((bf16[64,8,1280]{2,1,0:T(8,128)(2,1)}), bf16[64,8,1280]{2,1,0:T(8,128)(2,1)S(1)}, u32[]{:S(2)}, u32[]{:S(2)}) async-start(bf16[64,8,1280]{2,1,0:T(8,128)(2,1)} %gather_fusion.1), calls=%async_computation.3 | async-start | bytes 2621440 | tf_op jit(solution)/shard_map/all_to_all | solution.py:250
  99.7 36.9 %copy-start.9 = (bf16[256]{0:T(256)(128)(2,1)S(1)}, bf16[256]{0:T(256)(128)(2,1)}, u32[]{:S(2)}) copy-start(bf16[256]{0:T(256)(128)(2,1)} %param.14) | copy-start | bytes 1540
  99.7 37.0 %copy-start.10 = (bf16[256]{0:T(256)(128)(2,1)S(1)}, bf16[256]{0:T(256)(128)(2,1)}, u32[]{:S(2)}) copy-start(bf16[256]{0:T(256)(128)(2,1)} %param.15) | copy-start | bytes 1540
  99.7 37.0 %copy-start.7 = (bf16[2048]{0:T(1024)(128)(2,1)S(1)}, bf16[2048]{0:T(1024)(128)(2,1)}, u32[]{:S(2)}) copy-start(bf16[2048]{0:T(1024)(128)(2,1)} %param.13) | copy-start | bytes 12292
  99.7 37.0 %copy-start.11 = (s32[64]{0:T(128)S(1)}, s32[64]{0:T(128)}, u32[]{:S(2)}) copy-start(s32[64]{0:T(128)} %param.19) | copy-start | bytes 772
  131.1 39.9 %all-to-all-start.1 = ((bf16[64,8,1280]{2,1,0:T(8,128)(2,1)}), bf16[64,8,1280]{2,1,0:T(8,128)(2,1)S(1)}, u32[]{:S(2)}, u32[]{:S(2)}) async-start(bf16[64,8,1280]{2,1,0:T(8,128)(2,1)} %gather_fusion), calls=%async_computation.1 | async-start | bytes 2621440 | tf_op jit(solution)/shard_map/all_to_all | solution.py:250
  136.7 2.5 %copy-start = (bf16[2048,256]{1,0:T(8,128)(2,1)S(1)}, bf16[2048,256]{1,0:T(8,128)(2,1)}, u32[]{:S(2)}) copy-start(bf16[2048,256]{1,0:T(8,128)(2,1)} %cache_k.3) | copy-start | bytes 3145732
  136.7 2.5 %copy-start.2 = (bf16[2048,256]{1,0:T(8,128)(2,1)S(1)}, bf16[2048,256]{1,0:T(8,128)(2,1)}, u32[]{:S(2)}) copy-start(bf16[2048,256]{1,0:T(8,128)(2,1)} %cache_v.3) | copy-start | bytes 3145732
  171.0 1.2 copy-start.1
  172.2 1.2 copy-start.3

commit v3 on v1

--- a/solution.py
+++ b/solution.py
@@ -34,15 +34,22 @@
     return x * cosine + pltpu.roll(x, HEAD // 2, 1) * sine
 
 
+def packet_columns(q_width, k_width):
+    half = q_width // 2
+    return 0, half, half + k_width, half + 2 * k_width
+
+
 def attention_kernel(
     length_ref, tok, q_bias, k_bias, v_bias, cache_k, cache_v, cosine, sine,
     out, new_keys, new_values, stats,
     keys, values, s_a, s_b, m_a, m_b,
 ):
-    rows = tok.shape[1]
-    kv_count = tok.shape[0]
+    pieces, tall, _ = tok.shape
+    rows = pieces * tall
+    kv_count = k_bias.shape[1] // HEAD
     cached = cache_k.shape[0]
-    group = tok.shape[2] // HEAD - 2
+    group = q_bias.shape[1] // HEAD // kv_count
+    _, k_at, v_at, _ = packet_columns(q_bias.shape[1], k_bias.shape[1])
     half = 256
     halves = rows // half
     length = length_ref[0]
@@ -52,6 +59,10 @@
     causal = lax.broadcasted_iota(jnp.int32, (half, half), 1) <= lax.broadcasted_iota(
         jnp.int32, (half, half), 0
     )
+
+    def arrived(first, count, at):
+        x = tok[first // tall : (first + count) // tall, :, at].astype(jnp.float32)
+        return x.reshape(count, HEAD)
 
     def prepare(kv):
         at = slice(kv * HEAD, (kv + 1) * HEAD)
@@ -59,12 +70,12 @@
         keys[:cached, :] = jnp.where(valid, cache_k[:, at], cache_k[0:1, at])
         values[:cached, :HEAD] = jnp.where(valid, cache_v[:, at], jnp.bfloat16(0))
         values[:cached, HEAD:] = jnp.where(valid, jnp.bfloat16(1), jnp.bfloat16(0))
-        fresh = tok[kv, :, group * HEAD : (group + 1) * HEAD].astype(jnp.float32)
+        fresh = arrived(0, rows, slice(k_at + kv * HEAD, k_at + (kv + 1) * HEAD))
         fresh = fresh + k_bias[0:1, at].astype(jnp.float32)
         fresh = rope(fresh, cosine[...], sine[...]).astype(jnp.bfloat16)
         keys[cached:, :] = fresh
         new_keys[:, at] = fresh
-        fresh = tok[kv, :, (group + 1) * HEAD :].astype(jnp.float32)
+        fresh = arrived(0, rows, slice(v_at + kv * HEAD, v_at + (kv + 1) * HEAD))
         fresh = (fresh + v_bias[0:1, at].astype(jnp.float32)).astype(jnp.bfloat16)
         values[cached:, :HEAD] = fresh
         values[cached:, HEAD:] = jnp.ones((rows, HEAD), jnp.bfloat16)
@@ -76,12 +87,13 @@
         return blocks
 
     def score(kv, head, s_ref, m_ref):
-        at = pl.ds(pl.multiple_of(head * HEAD, HEAD), HEAD)
+        q_at = packet_columns(q_bias.shape[1], k_bias.shape[1])[0 if kv == 0 else 3]
+        at = pl.ds(pl.multiple_of(q_at + head * HEAD, HEAD), HEAD)
         bias_at = pl.ds(pl.multiple_of((kv * group + head) * HEAD, HEAD), HEAD)
         bias = q_bias[0:1, bias_at].astype(jnp.float32)
         for part in range(halves):
             here = slice(part * half, (part + 1) * half)
-            x = tok[kv, here, at].astype(jnp.float32) + bias
+            x = arrived(part * half, half, at) + bias
             query = rope(x, cosine[here, :], sine[here, :]).astype(jnp.bfloat16)
             largest = None
             for first, masked in key_blocks(part):
@@ -136,7 +148,8 @@
 
 
 def attend(length, tok, q_bias, k_bias, v_bias, cache_k, cache_v, cosine, sine):
-    kv_count, rows, _ = tok.shape
+    rows = tok.shape[0] * tok.shape[1]
+    kv_count = k_bias.shape[0] // HEAD
     cached = cache_k.shape[0]
     vmem = pl.BlockSpec(memory_space=pltpu.VMEM)
     return pl.pallas_call(
@@ -211,40 +224,86 @@
     return out[0, 0:1], out[1, 0:1]
 
 
-def split_kv(q, k, v):
-    kv_count = k.shape[1] // HEAD
-    wide = q.shape[1] // kv_count
-    return jnp.stack(
-        [
-            jnp.concatenate(
-                [
-                    q[:, i * wide : (i + 1) * wide],
-                    k[:, i * HEAD : (i + 1) * HEAD],
-                    v[:, i * HEAD : (i + 1) * HEAD],
-                ],
-                axis=1,
-            )
-            for i in range(kv_count)
-        ]
-    )
-
-
-def exchange(tok, deal):
+def exchange_kernel(n, parts, *refs):
+    *sources, out, send_sem, recv_sem, own_sems = refs
+    me = lax.axis_index("seq")
+    barrier = pltpu.get_barrier_semaphore()
+
+    def greet(step, carry):
+        pl.semaphore_signal(barrier, inc=1, device_id={"seq": lax.rem(me + step, n)}, device_id_type=MESH)
+        return carry
+
+    lax.fori_loop(1, n, greet, 0)
+    pl.semaphore_wait(barrier, n - 1)
+
+    def send(peer):
+        for source, first, width, to in parts:
+            pltpu.make_async_remote_copy(
+                src_ref=sources[source].at[peer, :, first : first + width],
+                dst_ref=out.at[me, :, to : to + width],
+                send_sem=send_sem, recv_sem=recv_sem,
+                device_id={"seq": peer}, device_id_type=MESH,
+            ).start()
+
+    def send_both_ways(step, carry):
+        send(lax.rem(me + step, n))
+        send(lax.rem(me + n - step, n))
+        return carry
+
+    lax.fori_loop(1, n // 2, send_both_ways, 0)
+    send(lax.rem(me + n // 2, n))
+    own = [
+        pltpu.make_async_copy(
+            sources[source].at[me, :, first : first + width],
+            out.at[me, :, to : to + width], own_sems.at[i],
+        )
+        for i, (source, first, width, to) in enumerate(parts)
+    ]
+    for copy in own:
+        copy.start()
+    for copy in own:
+        copy.wait()
+    others = out.at[pl.ds(0, n - 1)]
+    pltpu.make_async_copy(others, others, recv_sem).wait()
+    pltpu.make_async_copy(others, others, send_sem).wait()
+
+
+def exchange(parts, width, collective_id, *sources):
+    n = lax.axis_size("seq")
+    anywhere = pl.BlockSpec(memory_space=pl.ANY)
+    return pl.pallas_call(
+        functools.partial(exchange_kernel, n, parts),
+        out_shape=jax.ShapeDtypeStruct((n, sources[0].shape[1], width), jnp.bfloat16),
+        in_specs=[anywhere] * len(sources),
+        out_specs=anywhere,
+        scratch_shapes=[
+            pltpu.SemaphoreType.DMA, pltpu.SemaphoreType.DMA,
+            pltpu.SemaphoreType.DMA((len(parts),)),
+        ],
+        compiler_params=pltpu.CompilerParams(collective_id=collective_id, has_side_effects=True),
+        name="exchange",
+    )(*sources)
+
+
+def deliver(q, k, v, deal):
     slots = lax.axis_size("seq")
     slot_ids = jnp.arange(slots, dtype=jnp.int32)
     inverse = jnp.sum(jnp.where(deal[None, :] == slot_ids[:, None], slot_ids[None, :], 0), axis=1)
-    flat = tok.reshape(slots, -1, tok.shape[2])
-    spread = lax.all_to_all(flat, "seq", split_axis=0, concat_axis=0, tiled=True)
-    picked = jnp.take(spread, inverse, axis=0)
-    settled = lax.all_to_all(picked, "seq", split_axis=0, concat_axis=0, tiled=True)
-    return settled.reshape(tok.shape)
+    half, k_width = q.shape[1] // 2, k.shape[1]
+    width = q.shape[1] + 2 * k_width
+    first_at, k_at, v_at, second_at = packet_columns(q.shape[1], k_width)
+    q, k, v = (x.reshape(slots, -1, x.shape[1]) for x in (q, k, v))
+    parts = ((0, 0, half, first_at), (1, 0, k_width, k_at), (2, 0, k_width, v_at), (0, half, half, second_at))
+    spread = exchange(parts, width, 2, q, k, v)
+    picked = jnp.take(spread, inverse, axis=0, mode="clip")
+    return exchange(((0, 0, width, 0),), width, 3, picked)
 
 
 def body(q_new, k_new, v_new, q_bias, k_bias, v_bias, cache_k, cache_v, deal, cache_len):
     rows = q_new.shape[0]
     length = cache_len[lax.axis_index("seq")]
     cosine, sine = tables(length, rows)
-    tok = exchange(split_kv(q_new, k_new, v_new), deal)
+    tok = deliver(q_new, k_new, v_new, deal)
     attn_out, new_keys, new_values, stats = attend(
         length, tok, q_bias, k_bias, v_bias, cache_k, cache_v, cosine, sine
     )

time: 192 us -> 188 us (0.979)
  Pallas kernels: 33.3 us -> 171 us
  waiting for transfers between devices: 122 us -> 0 us
  starting transfers between devices: 17.7 us -> 0 us
  other arithmetic: 7.49 us -> 2.62 us
    pallas_call x0 -> x2, Pallas kernels: none -> 138 us  [exchange(): pl.pallas_call(functools.partial(exchange_kernel, n, parts), out_shape=ja...]
    all_to_all x2 -> x0, waiting for transfers between devices: 122 us -> none  [the longest x1 62.4 us: exchange(): lax.all_to_all(flat, 'seq', split_axis=0, concat_axis=0, tiled=True)]
    all_to_all x2 -> x0, starting transfers between devices: 17.7 us -> none  [the longest x1 12.1 us: exchange(): lax.all_to_all(flat, 'seq', split_axis=0, concat_axis=0, tiled=True)]
    select_n x2 -> x0, other arithmetic: 3.54 us -> none  [exchange(): picked = jnp.take(spread, inverse, axis=0)]
    another operation x2 -> x0, other arithmetic: 1.97 us -> none  [split_kv(): jnp.stack([jnp.concatenate([q[:, i * wide:(i + 1) * wide], k[:, i * HEAD:...]
  transfers between devices with their start and end apart: 2 -> 0, of which waited for: 2 -> 0; matrix products, arithmetic and copies ran while one was open for 1% -> 0% of each run, Pallas kernels for 0% -> 0%
where the time goes in v3:
time: 188 us; the launch traced here: 186 us
  Pallas kernels  171 us (91%)
  local copies, waits for them, and re-layouts  10.8 us (6%)
  other arithmetic  2.62 us (1%)
    pallas_call x2, Pallas kernels, exchange(): pl.pallas_call(functools.partial(exchange_kernel, n, parts), out_shape=ja...  138 us
    pallas_call x1, Pallas kernels, attend(): pl.pallas_call(attention_kernel, out_shape=(jax.ShapeDtypeStruct((rows, q...  26.7 us
    pallas_call x1, Pallas kernels, reduce_stats(): pl.pallas_call(functools.partial(stats_kernel, n, width), out_shape=jax.S...  6.56 us
    gather x1, local copies, waits for them, and re-layouts, deliver(): picked = jnp.take(spread, inverse, axis=0, mode='clip')  3.97 us

profile of v3, /device:TPU:18, one launch (start us, length us, event | category | flops | bytes accessed | tf_op | source)
XLA Modules:
  0.0 185.6 jit_solution(8574895683009446045)
XLA Ops:
  0.6 1.2 dynamic_slice.3.length_ref
  1.9 0.8 select_reduce_fusion
  2.7 0.7 reshape.43.k_bias
  3.3 0.7 reshape.44.v_bias
  4.0 0.6 add_convert_fusion
  4.7 0.7 reshape.42.q_bias
  5.3 1.0 fusion
  6.3 0.2 pad_maximum_fusion
  6.6 68.6 %exchange.2 = bf16[64,8,2560]{2,1,0:T(8,128)(2,1)} custom-call(bf16[64,8,2048]{2,1,0:T(8,128)(2,1)} %bitcast.6, bf16[64,8,256]{2,1,0:T(8,128)(2,1)} %bitcast.7, bf16[64,8,256]{2,1,0:T(8,128)(2,1)} %bitcast.8), custom_call_target="tpu_custom_call" | custom-call | tf_op jit(solution)/shard_map/exchange/pallas_call | solution.py:274
  75.1 4.0 %gather_fusion = bf16[64,8,2560]{2,1,0:T(8,128)(2,1)} fusion(bf16[64,8,2560]{2,1,0:T(8,128)(2,1)} %exchange.2, s32[1024]{0:T(1024)S(1)} %pad_clamp_fusion), kind=kCustom, calls=%fused_computation | custom fusion | bytes 5243136 | tf_op jit(solution)/shard_map/jit(_take)/gather | solution.py:298
  79.1 0.0 copy-start.1
  79.1 0.0 copy-start.2
  79.1 69.6 %exchange.3.tok = bf16[64,8,2560]{2,1,0:T(8,128)(2,1)} custom-call(bf16[64,8,2560]{2,1,0:T(8,128)(2,1)} %gather_fusion), custom_call_target="tpu_custom_call" | custom-call | tf_op jit(solution)/shard_map/exchange/pallas_call | solution.py:274
  148.7 0.0 copy-done.1
  148.7 0.0 copy-done.2
  148.7 0.0 copy-start
  148.7 1.7 copy-done
  150.5 26.7 %attention.1 = (bf16[512,2048]{1,0:T(8,128)(2,1)}, bf16[512,256]{1,0:T(8,128)(2,1)}, bf16[512,256]{1,0:T(8,128)(2,1)}, f32[8,128]{1,0:T(8,128)S(1)}) custom-call(s32[1]{0:T(128)} %dynamic_slice.3.length_ref, bf16[64,8,2560]{2,1,0:T(8,128)(2,1)S(1)} %copy-done, bf16[1,2048]{1,0:T(2,128)(2,1)S(1)} %reshape.42.q_bias, bf16[1,256]{1,0:T(2,128)(2,1)S(1)} %reshape.43.k_bias, ...), custom_call_target="tpu_custom_call" | custom-call | tf_op jit(solution)/shard_map/attention/pallas_call | solution.py:155
  177.1 0.0 copy-start.3
  177.1 0.6 copy-done.3
  177.7 6.6 %stats.1 = f32[8,128]{1,0:T(8,128)} custom-call(f32[8,128]{1,0:T(8,128)} %copy-done.3), custom_call_target="tpu_custom_call" | custom-call | tf_op jit(solution)/shard_map/stats/pallas_call | solution.py:211
  184.3 1.3 fusion.1
  (2 shorter events, 0.0 us)
Async XLA Ops:
  79.1 69.6 %copy-start.1 = (bf16[2048,256]{1,0:T(8,128)(2,1)S(1)}, bf16[2048,256]{1,0:T(8,128)(2,1)}, u32[]{:S(2)}) copy-start(bf16[2048,256]{1,0:T(8,128)(2,1)} %cache_k.1) | copy-start | bytes 3145732
  79.1 69.6 %copy-start.2 = (bf16[2048,256]{1,0:T(8,128)(2,1)S(1)}, bf16[2048,256]{1,0:T(8,128)(2,1)}, u32[]{:S(2)}) copy-start(bf16[2048,256]{1,0:T(8,128)(2,1)} %cache_v.1) | copy-start | bytes 3145732
  148.7 1.7 copy-start
  177.1 0.6 copy-start.3

commit v4 on v3

--- a/solution.py
+++ b/solution.py
@@ -39,13 +39,46 @@
     return 0, half, half + k_width, half + 2 * k_width
 
 
+def greet_all(n):
+    me = lax.axis_index("seq")
+    barrier = pltpu.get_barrier_semaphore()
+
+    def greet(step, carry):
+        pl.semaphore_signal(barrier, inc=1, device_id={"seq": lax.rem(me + step, n)}, device_id_type=MESH)
+        return carry
+
+    lax.fori_loop(1, n, greet, 0)
+    pl.semaphore_wait(barrier, n - 1)
+    return me
+
+
+def send_all(n, me, parts, out, send_sem, recv_sem):
+    def send(peer):
+        for source, first, width, to in parts:
+            pltpu.make_async_remote_copy(
+                src_ref=source.at[peer, :, first : first + width],
+                dst_ref=out.at[me, :, to : to + width],
+                send_sem=send_sem, recv_sem=recv_sem,
+                device_id={"seq": peer}, device_id_type=MESH,
+            ).start()
+
+    def send_both_ways(step, carry):
+        send(lax.rem(me + step, n))
+        send(lax.rem(me + n - step, n))
+        return carry
+
+    lax.fori_loop(1, n // 2, send_both_ways, 0)
+    send(lax.rem(me + n // 2, n))
+
+
 def attention_kernel(
-    length_ref, tok, q_bias, k_bias, v_bias, cache_k, cache_v, cosine, sine,
+    n, length_ref, picked, q_bias, k_bias, v_bias, cache_k, cache_v, cosine, sine,
     out, new_keys, new_values, stats,
-    keys, values, s_a, s_b, m_a, m_b,
+    tok, keys, values, s_a, s_b, m_a, m_b, send_sems, recv_sems, own_sems,
 ):
-    pieces, tall, _ = tok.shape
+    pieces, tall, width = tok.shape
     rows = pieces * tall
+    me = greet_all(n)
     kv_count = k_bias.shape[1] // HEAD
     cached = cache_k.shape[0]
     group = q_bias.shape[1] // HEAD // kv_count
@@ -54,6 +87,24 @@
     halves = rows // half
     length = length_ref[0]
 
+    first_chunk = packet_columns(q_bias.shape[1], k_bias.shape[1])[3]
+    chunks = (slice(0, first_chunk), slice(first_chunk, width))
+    for i, at in enumerate(chunks):
+        send_all(
+            n, me, [(picked, at.start, at.stop - at.start, at.start)], tok,
+            send_sems.at[i], recv_sems.at[i],
+        )
+    own = [
+        pltpu.make_async_copy(picked.at[me, :, at], tok.at[me, :, at], own_sems.at[i])
+        for i, at in enumerate(chunks)
+    ]
+    for copy in own:
+        copy.start()
+
+    def wait_for(i, sems):
+        others = tok.at[pl.ds(0, n - 1), :, chunks[i]]
+        pltpu.make_async_copy(others, others, sems.at[i]).wait()
+
     stats[...] = jnp.zeros_like(stats)
     stats[1:2, :] = jnp.full((1, HEAD), low_score, jnp.float32)
     causal = lax.broadcasted_iota(jnp.int32, (half, half), 1) <= lax.broadcasted_iota(
@@ -64,12 +115,15 @@
         x = tok[first // tall : (first + count) // tall, :, at].astype(jnp.float32)
         return x.reshape(count, HEAD)
 
-    def prepare(kv):
+    def prepare_cached(kv):
         at = slice(kv * HEAD, (kv + 1) * HEAD)
         valid = lax.broadcasted_iota(jnp.int32, (cached, HEAD), 0) < length
         keys[:cached, :] = jnp.where(valid, cache_k[:, at], cache_k[0:1, at])
         values[:cached, :HEAD] = jnp.where(valid, cache_v[:, at], jnp.bfloat16(0))
         values[:cached, HEAD:] = jnp.where(valid, jnp.bfloat16(1), jnp.bfloat16(0))
+
+    def prepare_new(kv):
+        at = slice(kv * HEAD, (kv + 1) * HEAD)
         fresh = arrived(0, rows, slice(k_at + kv * HEAD, k_at + (kv + 1) * HEAD))
         fresh = fresh + k_bias[0:1, at].astype(jnp.float32)
         fresh = rope(fresh, cosine[...], sine[...]).astype(jnp.bfloat16)
@@ -132,7 +186,10 @@
                 stats[1:2, :] = jnp.maximum(stats[1:2, :], m[half - 1 : half, :] * scale)
 
     for kv in range(kv_count):
-        prepare(kv)
+        prepare_cached(kv)
+        own[kv].wait()
+        wait_for(kv, recv_sems)
+        prepare_new(kv)
         score(kv, 0, s_a, m_a)
 
         @pl.loop(0, group // 2 - 1)
@@ -145,35 +202,43 @@
         score(kv, group - 1, s_b, m_b)
         mix(kv, group - 2, s_a, m_a)
         mix(kv, group - 1, s_b, m_b)
-
-
-def attend(length, tok, q_bias, k_bias, v_bias, cache_k, cache_v, cosine, sine):
-    rows = tok.shape[0] * tok.shape[1]
+    for i in range(len(chunks)):
+        wait_for(i, send_sems)
+
+
+def attend(length, picked, q_bias, k_bias, v_bias, cache_k, cache_v, cosine, sine):
+    rows = picked.shape[0] * picked.shape[1]
     kv_count = k_bias.shape[0] // HEAD
     cached = cache_k.shape[0]
     vmem = pl.BlockSpec(memory_space=pltpu.VMEM)
     return pl.pallas_call(
-        attention_kernel,
+        functools.partial(attention_kernel, picked.shape[0]),
         out_shape=(
             jax.ShapeDtypeStruct((rows, q_bias.shape[0]), jnp.bfloat16),
             jax.ShapeDtypeStruct((rows, kv_count * HEAD), jnp.bfloat16),
             jax.ShapeDtypeStruct((rows, kv_count * HEAD), jnp.bfloat16),
             jax.ShapeDtypeStruct((8, HEAD), jnp.float32),
         ),
-        in_specs=[pl.BlockSpec(memory_space=pltpu.SMEM)] + [vmem] * 8,
+        in_specs=[pl.BlockSpec(memory_space=pltpu.SMEM), pl.BlockSpec(memory_space=pl.ANY)] + [vmem] * 7,
         out_specs=[vmem] * 4,
         scratch_shapes=[
+            pltpu.VMEM(picked.shape, jnp.bfloat16),
             pltpu.VMEM((cached + rows, HEAD), jnp.bfloat16),
             pltpu.VMEM((cached + rows, 2 * HEAD), jnp.bfloat16),
             pltpu.VMEM((rows, cached + rows), jnp.float32),
             pltpu.VMEM((rows, cached + rows), jnp.float32),
             pltpu.VMEM((rows, HEAD), jnp.float32),
             pltpu.VMEM((rows, HEAD), jnp.float32),
+            pltpu.SemaphoreType.DMA((2,)),
+            pltpu.SemaphoreType.DMA((2,)),
+            pltpu.SemaphoreType.DMA((2,)),
         ],
-        compiler_params=pltpu.CompilerParams(vmem_limit_bytes=48 << 20),
+        compiler_params=pltpu.CompilerParams(
+            vmem_limit_bytes=48 << 20, collective_id=3, has_side_effects=True
+        ),
         name="attention",
     )(
-        length.reshape(1), tok, q_bias.reshape(1, -1), k_bias.reshape(1, -1),
+        length.reshape(1), picked, q_bias.reshape(1, -1), k_bias.reshape(1, -1),
         v_bias.reshape(1, -1), cache_k, cache_v, cosine, sine,
     )
 
@@ -226,32 +291,8 @@
 
 def exchange_kernel(n, parts, *refs):
     *sources, out, send_sem, recv_sem, own_sems = refs
-    me = lax.axis_index("seq")
-    barrier = pltpu.get_barrier_semaphore()
-
-    def greet(step, carry):
-        pl.semaphore_signal(barrier, inc=1, device_id={"seq": lax.rem(me + step, n)}, device_id_type=MESH)
-        return carry
-
-    lax.fori_loop(1, n, greet, 0)
-    pl.semaphore_wait(barrier, n - 1)
-
-    def send(peer):
-        for source, first, width, to in parts:
-            pltpu.make_async_remote_copy(
-                src_ref=sources[source].at[peer, :, first : first + width],
-                dst_ref=out.at[me, :, to : to + width],
-                send_sem=send_sem, recv_sem=recv_sem,
-                device_id={"seq": peer}, device_id_type=MESH,
-            ).start()
-
-    def send_both_ways(step, carry):
-        send(lax.rem(me + step, n))
-        send(lax.rem(me + n - step, n))
-        return carry
-
-    lax.fori_loop(1, n // 2, send_both_ways, 0)
-    send(lax.rem(me + n // 2, n))
+    me = greet_all(n)
+    send_all(n, me, [(sources[source], *rest) for source, *rest in parts], out, send_sem, recv_sem)
     own = [
         pltpu.make_async_copy(
             sources[source].at[me, :, first : first + width],
@@ -285,7 +326,7 @@
     )(*sources)
 
 
-def deliver(q, k, v, deal):
+def spread_pieces(q, k, v, deal):
     slots = lax.axis_size("seq")
     slot_ids = jnp.arange(slots, dtype=jnp.int32)
     inverse = jnp.sum(jnp.where(deal[None, :] == slot_ids[:, None], slot_ids[None, :], 0), axis=1)
@@ -295,17 +336,16 @@
     q, k, v = (x.reshape(slots, -1, x.shape[1]) for x in (q, k, v))
     parts = ((0, 0, half, first_at), (1, 0, k_width, k_at), (2, 0, k_width, v_at), (0, half, half, second_at))
     spread = exchange(parts, width, 2, q, k, v)
-    picked = jnp.take(spread, inverse, axis=0, mode="clip")
-    return exchange(((0, 0, width, 0),), width, 3, picked)
+    return jnp.take(spread, inverse, axis=0, mode="clip")
 
 
 def body(q_new, k_new, v_new, q_bias, k_bias, v_bias, cache_k, cache_v, deal, cache_len):
     rows = q_new.shape[0]
     length = cache_len[lax.axis_index("seq")]
     cosine, sine = tables(length, rows)
-    tok = deliver(q_new, k_new, v_new, deal)
+    picked = spread_pieces(q_new, k_new, v_new, deal)
     attn_out, new_keys, new_values, stats = attend(
-        length, tok, q_bias, k_bias, v_bias, cache_k, cache_v, cosine, sine
+        length, picked, q_bias, k_bias, v_bias, cache_k, cache_v, cosine, sine
     )
     last_norm, top_logit = reduce_stats(stats, q_new.shape[1] * lax.axis_size("tp"))
     return attn_out, new_keys, new_values, last_norm, top_logit

time: 188 us -> 177 us (0.941)
  Pallas kernels: 171 us -> 156 us
  local copies, waits for them, and re-layouts: 10.8 us -> 15.5 us
    pallas_call x2 -> x1, Pallas kernels: 138 us -> 68.2 us  [exchange(): pl.pallas_call(functools.partial(exchange_kernel, n, parts), out_shape=ja...]
    pallas_call x1, Pallas kernels: 26.7 us -> 81.4 us  [attend(): pl.pallas_call(functools.partial(attention_kernel, picked.shape[0]), out_...]
    unnamed x8 -> x19, local copies, waits for them, and re-layouts: 2.33 us -> 6.9 us
where the time goes in v4:
time: 177 us; the launch traced here: 176 us
  Pallas kernels  156 us (88%)
  local copies, waits for them, and re-layouts  15.5 us (9%)
  other arithmetic  3.31 us (2%)
    pallas_call x1, Pallas kernels, attend(): pl.pallas_call(functools.partial(attention_kernel, picked.shape[0]), out_...  81.4 us
    pallas_call x1, Pallas kernels, exchange(): pl.pallas_call(functools.partial(exchange_kernel, n, parts), out_shape=ja...  68.2 us
    unnamed x19, local copies, waits for them, and re-layouts  6.9 us
    pallas_call x1, Pallas kernels, reduce_stats(): pl.pallas_call(functools.partial(stats_kernel, n, width), out_shape=jax.S...  6.62 us
    gather x1, local copies, waits for them, and re-layouts, spread_pieces(): return jnp.take(spread, inverse, axis=0, mode='clip')  4.04 us

profile of v4, /device:TPU:18, one launch (start us, length us, event | category | flops | bytes accessed | tf_op | source)
XLA Modules:
  0.0 175.7 jit_solution(38151918848881220)
XLA Ops:
  0.6 1.2 dynamic_slice.3.length_ref
  1.9 0.8 select_reduce_fusion
  2.7 0.7 reshape.43.k_bias
  3.3 0.7 reshape.44.v_bias
  4.0 0.6 add_convert_fusion
  4.7 0.7 reshape.42.q_bias
  5.3 1.0 fusion
  6.3 0.9 pad_maximum_fusion
  7.2 68.2 %exchange.1 = bf16[64,8,2560]{2,1,0:T(8,128)(2,1)} custom-call(bf16[64,8,2048]{2,1,0:T(8,128)(2,1)} %bitcast.6, bf16[64,8,256]{2,1,0:T(8,128)(2,1)} %bitcast.7, bf16[64,8,256]{2,1,0:T(8,128)(2,1)} %bitcast.8), custom_call_target="tpu_custom_call" | custom-call | tf_op jit(solution)/shard_map/exchange/pallas_call | solution.py:315
  75.4 0.0 copy-start
  75.5 4.0 %gather_fusion = bf16[64,8,2560]{2,1,0:T(8,128)(2,1)} fusion(bf16[64,8,2560]{2,1,0:T(8,128)(2,1)} %exchange.1, s32[1024]{0:T(1024)S(1)} %pad_clamp_fusion), kind=kCustom, calls=%fused_computation | custom fusion | bytes 5243136 | tf_op jit(solution)/shard_map/jit(_take)/gather | solution.py:339
  79.5 0.0 copy-done
  79.5 0.0 copy-start.1
  79.5 1.2 copy-done.1
  80.7 0.0 copy-start.2
  80.7 0.9 copy-done.2
  81.7 81.4 %attention.1 = (bf16[512,2048]{1,0:T(8,128)(2,1)S(1)}, bf16[512,256]{1,0:T(8,128)(2,1)S(1)}, bf16[512,256]{1,0:T(8,128)(2,1)S(1)}, f32[8,128]{1,0:T(8,128)S(1)}) custom-call(s32[1]{0:T(128)} %dynamic_slice.3.length_ref, bf16[64,8,2560]{2,1,0:T(8,128)(2,1)} %gather_fusion, bf16[1,2048]{1,0:T(2,128)(2,1)S(1)} %reshape.42.q_bias, ...), custom_call_target="tpu_custom_call" | custom-call | tf_op jit(solution)/shard_map/attention/pallas_call | solution.py:214
  163.1 0.0 copy-start.3
  163.1 0.7 copy-done.3
  163.8 0.0 copy-start.5
  163.8 0.7 copy-done.5
  164.5 0.0 copy-start.7
  164.5 0.6 copy-done.7
  165.1 0.0 copy-start.6
  165.1 0.0 copy-start.4
  165.1 6.6 %stats.1 = f32[8,128]{1,0:T(8,128)} custom-call(f32[8,128]{1,0:T(8,128)} %copy-done.7), custom_call_target="tpu_custom_call" | custom-call | tf_op jit(solution)/shard_map/stats/pallas_call | solution.py:276
  171.7 1.3 fusion.1
  173.0 1.3 copy.18
  174.3 0.0 copy-done.6
  174.3 0.7 copy.19
  175.0 0.0 copy-done.4
  175.0 0.7 copy.20
  (2 shorter events, 0.0 us)
Async XLA Ops:
  75.4 4.1 %copy-start = (bf16[2048,256]{1,0:T(8,128)(2,1)S(1)}, bf16[2048,256]{1,0:T(8,128)(2,1)}, u32[]{:S(2)}) copy-start(bf16[2048,256]{1,0:T(8,128)(2,1)} %cache_k.1) | copy-start | bytes 3145732
  79.5 1.2 copy-start.1
  80.7 0.9 copy-start.2
  163.1 0.7 copy-start.3
  163.8 0.7 copy-start.5
  164.5 0.6 copy-start.7
  165.1 9.2 %copy-start.6 = (bf16[512,256]{1,0:T(8,128)(2,1)S(1)}, bf16[512,256]{1,0:T(8,128)(2,1)}, u32[]{:S(2)}) copy-start(bf16[512,256]{1,0:T(8,128)(2,1)} %copy-done.5) | copy-start | bytes 786436
  165.1 9.9 %copy-start.4 = (bf16[512,256]{1,0:T(8,128)(2,1)S(1)}, bf16[512,256]{1,0:T(8,128)(2,1)}, u32[]{:S(2)}) copy-start(bf16[512,256]{1,0:T(8,128)(2,1)} %copy-done.3) | copy-start | bytes 786436
